TPU v7x, 768 devices: a whole 4x8x12 slice. The times are simulated.
768 devices in a mesh: band: 32 (over x, y), field: 24 (over z, core).
Axes of the slice: x: 4, y: 8, z: 12, core: 2. Of those that a mesh axis runs over, the one named last changes fastest.
Arguments:
- fourier: bfloat16 [768, 192, 1792], P(None, 'field', 'band'), may hold values from -6 to 6
- quad_weights: float32 [1792], P('band'), may hold values from 0.1 to 1.9
- legendre: bfloat16 [768, 1792, 768], P(('band', 'field')), may hold values from -0.125 to 0.125
- slot_wave: int32 [768], replicated, may hold values from 0 to 767, each once
- vert_proj: float32 [96, 96], replicated, may hold values from -0.625 to 0.625
- vert_recon: float32 [96, 96], replicated, may hold values from -0.625 to 0.625
- vert_rates: float32 [96], replicated, may hold values from 0.3 to 30
Outputs:
- spectral: bfloat16 [768, 2, 96, 768], P(('band', 'field'))
- returned: bfloat16 [768, 192, 1792], P(None, 'field', 'band')
Inputs may be any that keep to these rules, and one draw needn't show every extreme that they name: `slot_wave`: every wavenumber 0 .. 767 stands in exactly one slot.
All inputs are finite; a program needn't handle non-finite values.
Results may differ from a plain program's by a relative error of at most 0.0056.
Values may be sent and summed in bfloat16 or wider, within the bound.
A program may use at most 32 MiB of HBM per device.

v0:
```python
import jax
import jax.numpy as jnp
from jax import lax
from jax.sharding import PartitionSpec as P

LEV = 96


def damping(vert_rates, total):
    order = jnp.arange(total).astype(jnp.float32)
    growth = order * (order + 1.0) / float(total * total)
    return 1.0 / (1.0 + vert_rates[:, None] * growth[None, :])


def forward_block(data, block):
    return jnp.einsum("kal,kln->kan", data, block, preferred_element_type=jnp.float32)


def pick_rows(weighted, order):
    flat = weighted.reshape(weighted.shape[0], -1)
    return flat[order].reshape(weighted.shape)


def per_device(fourier, quad_weights, legendre, slot_wave, vert_proj, vert_recon, vert_rates):
    n_field = lax.axis_size("field")
    per_dev = legendre.shape[0]
    total = legendre.shape[2]
    weighted = (fourier.astype(jnp.float32) * quad_weights).astype(jnp.bfloat16)
    moved = lax.all_to_all(
        lax.all_to_all(
            pick_rows(weighted, slot_wave), "band", split_axis=0, concat_axis=2, tiled=True
        ),
        "field",
        split_axis=0,
        concat_axis=1,
        tiled=True,
    )
    me = lax.axis_index("band") * n_field + lax.axis_index("field")
    my_waves = lax.dynamic_slice_in_dim(slot_wave, me * per_dev, per_dev)
    direct = forward_block(moved, legendre)
    gamma = damping(vert_rates, total)
    direct = direct.reshape(per_dev, 2, LEV, total)
    modes = jnp.einsum("jl,kcln->kcjn", vert_proj, direct, precision=lax.Precision.HIGHEST) * gamma
    solved = jnp.einsum("lj,kcjn->kcln", vert_recon, modes, precision=lax.Precision.HIGHEST)
    keep = (jnp.arange(total)[None, :] >= my_waves[:, None]).astype(jnp.float32)
    spectral = (solved * keep[:, None, None, :]).astype(jnp.bfloat16)
    flat = spectral.reshape(per_dev, 2 * LEV, total)
    back = jnp.einsum("kan,kln->kal", flat, legendre, preferred_element_type=jnp.float32)
    back = back.astype(jnp.bfloat16)
    slots = jnp.arange(total)
    inverse = jnp.zeros((total,), jnp.int32).at[slot_wave].set(slots)
    first_back = lax.all_to_all(back, "field", split_axis=1, concat_axis=0, tiled=True)
    arrived = lax.all_to_all(first_back, "band", split_axis=2, concat_axis=0, tiled=True)
    returned = pick_rows(arrived, inverse)
    return (spectral, returned)


def solution(mesh):
    placed = (
        P(None, "field", "band"),
        P("band"),
        P(("band", "field"), None, None),
        P(),
        P(),
        P(),
        P(),
    )
    return jax.shard_map(
        per_device,
        mesh=mesh,
        in_specs=placed,
        out_specs=(P(("band", "field"), None, None, None), P(None, "field", "band")),
        check_vma=False,
    )
```

profile of v0, /device:TPU:8, one launch (start us, length us, event | category | flops | bytes accessed | tf_op | source)
XLA Modules:
  0.0 210.4 jit_solution(10500752031475253498)
XLA Ops:
  0.6 0.8 compare_select_fusion.1
  1.5 2.3 %multiply_convert_fusion = bf16[768,8,56]{0,2,1:T(8,128)(2,1)} fusion(bf16[768,8,56]{0,2,1:T(8,128)(2,1)} %param.7, f32[56]{0:T(128)} %param.8), kind=kLoop, calls=%fused_computation.9 | loop fusion | flops 1032192 | bytes 1376480 | tf_op jit(solution)/shard_map/convert_element_type | solution.py:28
  3.8 1.4 copy.40
  5.1 3.3 %gather_fusion = bf16[768,448]{1,0:T(8,128)(2,1)} fusion(bf16[768,448]{1,0:T(8,128)(2,1)S(1)} %copy.40, s32[1024]{0:T(1024)S(1)} %pad_clamp_fusion.1), kind=kCustom, calls=%fused_computation | custom fusion | bytes 1379328 | tf_op jit(solution)/shard_map/gather | solution.py:21
  8.4 1.4 copy.41
  9.8 1.9 copy.42
  11.7 4.3 %reshape.144 = bf16[32,2,5376]{2,1,0:T(2,128)(2,1)S(1)} reshape(bf16[768,8,56]{2,1,0:T(8,128)(2,1)} %copy.42) | data formatting | bytes 1376256
  16.0 31.1 %all_to_all.54 = bf16[32,2,5376]{2,1,0:T(2,128)(2,1)} all-to-all(bf16[32,2,5376]{2,1,0:T(2,128)(2,1)S(1)} %reshape.144), channel_id=1, replica_groups=mesh['band'=32,'field'=24] {'band'}, dimensions={0} | all-to-all | bytes 1376256 | tf_op jit(solution)/shard_map/all_to_all | solution.py:30
  47.1 5.2 %reshape.145 = bf16[768,8,56]{2,1,0:T(8,128)(2,1)} reshape(bf16[32,2,5376]{2,1,0:T(2,128)(2,1)} %all_to_all.54) | data formatting | bytes 1376256
  52.3 3.6 %copy.43 = bf16[24,8,32,56]{3,2,1,0:T(8,128)(2,1)} copy(bf16[24,8,32,56]{3,1,0,2:T(8,128)(2,1)} %bitcast.69) | data formatting | bytes 1376256 | tf_op jit(solution)/shard_map/all_to_all | solution.py:30
  55.9 4.0 %all_to_all.43 = bf16[24,8,1792]{2,1,0:T(8,128)(2,1)} reshape(bf16[24,8,32,56]{3,2,1,0:T(8,128)(2,1)} %copy.43) | data formatting | bytes 1376256 | tf_op jit(solution)/shard_map/all_to_all | solution.py:30
  59.8 15.5 %all-to-all-start.1 = ((bf16[24,8,1792]{2,1,0:T(8,128)(2,1)}), bf16[24,8,1792]{2,1,0:T(8,128)(2,1)S(1)}, u32[]{:S(2)}, u32[]{:S(2)}) async-start(bf16[24,8,1792]{2,1,0:T(8,128)(2,1)} %all_to_all.43), calls=%async_computation.1 | async-start | bytes 1376256 | tf_op jit(solution)/shard_map/all_to_all | solution.py:29
  75.3 1.3 dynamic_slice.3
  77.3 0.8 add_divide_fusion
  78.1 27.0 %all-to-all-done.1 = bf16[24,8,1792]{2,1,0:T(8,128)(2,1)S(1)} async-done(((bf16[24,8,1792]{2,1,0:T(8,128)(2,1)}), bf16[24,8,1792]{2,1,0:T(8,128)(2,1)S(1)}, u32[]{:S(2)}, u32[]{:S(2)}) %all-to-all-start.1) | async-done | bytes 688160 | tf_op jit(solution)/shard_map/all_to_all | solution.py:29
  108.1 1.1 fusion.7
  109.2 2.2 %copy.55 = bf16[1,192,1792]{2,0,1:T(2,128)(2,1)} copy(bf16[1,192,1792]{2,1,0:T(8,128)(2,1)S(1)} %fusion.7) | data formatting | bytes 1376256 | tf_op jit(solution)/shard_map/convert_element_type | solution.py:49
  111.9 5.8 %reduce = bf16[192,1792]{1,0:T(8,128)(2,1)S(1)} reduce(bf16[192,1,1792]{2,1,0:T(2,128)(2,1)} %bitcast.70, bf16[]{:T(256)} %broadcast.73), dimensions={1}, to_apply=%bitcast.65.reduce_sub_computation | reduce | bytes 1376258
  117.6 1.1 reshape.146
  118.7 33.8 %all_to_all.55 = bf16[24,2,7168]{2,1,0:T(2,128)(2,1)S(1)} all-to-all(bf16[24,2,7168]{2,1,0:T(2,128)(2,1)} %reshape.146), channel_id=1, replica_groups=mesh['band'=32,'field'=24] {'field'}, dimensions={0} | all-to-all | bytes 1376256 | tf_op jit(solution)/shard_map/all_to_all | solution.py:52
  152.5 1.9 reshape.147
  154.4 1.4 copy.54
  155.8 3.8 %copy.45 = bf16[24,8,1792]{0,1,2:T(8,128)(2,1)} copy(bf16[24,8,1792]{2,1,0:T(8,128)(2,1)S(1)} %bitcast.75) | data formatting | bytes 1376256 | tf_op jit(solution)/shard_map/all_to_all | solution.py:52
  159.6 6.6 %reshape.148 = bf16[32,2,5376]{2,1,0:T(2,128)(2,1)} reshape(bf16[1792,8,24]{2,1,0:T(8,128)(2,1)} %bitcast.68) | data formatting | bytes 1376256
  166.3 5.0 %all-to-all-start.3 = ((bf16[32,2,5376]{2,1,0:T(2,128)(2,1)}), bf16[32,2,5376]{2,1,0:T(2,128)(2,1)S(1)}, u32[]{:S(2)}, u32[]{:S(2)}) async-start(bf16[32,2,5376]{2,1,0:T(2,128)(2,1)} %reshape.148), calls=%async_computation.3 | async-start | bytes 1376256 | tf_op jit(solution)/shard_map/all_to_all | solution.py:53
  171.3 3.4 %scatter_custom_fusion = s32[768]{0:T(1024)S(1)} fusion(s32[768]{0:T(1024)S(1)} %compare_select_fusion.1, s32[768]{0:T(1024)S(1)} %iota.16, s32[]{:T(128)} %constant.7.clone.1), kind=kCustom, calls=%fused_computation.28 | custom fusion | bytes 3076 | tf_op jit(solution)/shard_map/scatter | solution.py:51
  174.7 16.2 %all-to-all-done.3 = bf16[32,2,5376]{2,1,0:T(2,128)(2,1)S(1)} async-done(((bf16[32,2,5376]{2,1,0:T(2,128)(2,1)}), bf16[32,2,5376]{2,1,0:T(2,128)(2,1)S(1)}, u32[]{:S(2)}, u32[]{:S(2)}) %all-to-all-start.3) | async-done | bytes 688160 | tf_op jit(solution)/shard_map/all_to_all | solution.py:53
  190.9 6.1 %reshape.149 = bf16[1792,8,24]{2,1,0:T(8,128)(2,1)} reshape(bf16[32,2,5376]{2,1,0:T(2,128)(2,1)S(1)} %all-to-all-done.3) | data formatting | bytes 1376256
  197.0 5.1 %copy.47 = bf16[32,24,8,56]{3,2,1,0:T(8,128)(2,1)} copy(bf16[32,24,8,56]{1,2,3,0:T(8,128)(2,1)} %bitcast.67) | data formatting | bytes 1376256 | tf_op jit(solution)/shard_map/all_to_all | solution.py:53
  202.1 2.8 %reshape.110 = bf16[768,448]{1,0:T(8,128)(2,1)S(1)} reshape(bf16[32,24,8,56]{3,2,1,0:T(8,128)(2,1)} %copy.47) | data formatting | bytes 1376256 | tf_op jit(solution)/shard_map/reshape | solution.py:20
  204.8 3.3 %gather_fusion.1 = bf16[768,448]{1,0:T(8,128)(2,1)} fusion(bf16[768,448]{1,0:T(8,128)(2,1)S(1)} %reshape.110, s32[1024]{0:T(1024)S(1)} %pad_clamp_fusion), kind=kCustom, calls=%fused_computation.1 | custom fusion | bytes 1379328 | tf_op jit(solution)/shard_map/gather | solution.py:21
  208.1 2.2 %copy.48 = bf16[768,448]{0,1:T(8,128)(2,1)} copy(bf16[768,448]{1,0:T(8,128)(2,1)} %gather_fusion.1) | data formatting | bytes 1376256 | tf_op jit(solution)/shard_map/gather | solution.py:21
  (22 shorter events, 4.2 us)
Async XLA Ops:
  0.6 104.4 %copy-start = (bf16[1,1792,768]{2,1,0:T(8,128)(2,1)S(1)}, bf16[1,1792,768]{2,1,0:T(8,128)(2,1)}, u32[]{:S(2)}) copy-start(bf16[1,1792,768]{2,1,0:T(8,128)(2,1)} %param.9) | copy-start | bytes 8257540
  55.9 21.4 %copy-start.5 = (f32[96]{0:T(128)S(1)}, f32[96]{0:T(128)}, u32[]{:S(2)}) copy-start(f32[96]{0:T(128)} %param.13) | copy-start | bytes 1156
  59.8 45.2 %all-to-all-start.1 = ((bf16[24,8,1792]{2,1,0:T(8,128)(2,1)}), bf16[24,8,1792]{2,1,0:T(8,128)(2,1)S(1)}, u32[]{:S(2)}, u32[]{:S(2)}) async-start(bf16[24,8,1792]{2,1,0:T(8,128)(2,1)} %all_to_all.43), calls=%async_computation.1 | async-start | bytes 1376256 | tf_op jit(solution)/shard_map/all_to_all | solution.py:29
  105.1 1.0 copy-start.2
  105.1 1.0 copy-start.3
  105.1 1.6 copy-start.4
  107.4 0.7 copy-start.1
  166.3 24.6 %all-to-all-start.3 = ((bf16[32,2,5376]{2,1,0:T(2,128)(2,1)}), bf16[32,2,5376]{2,1,0:T(2,128)(2,1)S(1)}, u32[]{:S(2)}, u32[]{:S(2)}) async-start(bf16[32,2,5376]{2,1,0:T(2,128)(2,1)} %reshape.148), calls=%async_computation.3 | async-start | bytes 1376256 | tf_op jit(solution)/shard_map/all_to_all | solution.py:53
where the time goes:
time: 211 us; the launch traced here: 210 us
  local copies, waits for them, and re-layouts  67.6 us (32%)
  blocking collectives  64.9 us (31%)
  waiting for transfers between devices  43.1 us (20%)
  starting transfers between devices  20.5 us (10%)
  other arithmetic  10.4 us (5%)
  matrix products  3.1 us (1%)
    all_to_all x1, blocking collectives, per_device(): lax.all_to_all(back, 'field', split_axis=1, concat_axis=0, tiled=True)  33.8 us
    all_to_all x1, blocking collectives, per_device(): lax.all_to_all(pick_rows(weighted, slot_wave), 'band', split_axis=0, conc...  31.1 us
    unnamed x20, local copies, waits for them, and re-layouts  28 us
    all_to_all x1, waiting for transfers between devices, per_device(): lax.all_to_all(lax.all_to_all(pick_rows(weighted, slot_wave), 'band', spl...  27 us
    all_to_all x1, waiting for transfers between devices, per_device(): lax.all_to_all(first_back, 'band', split_axis=2, concat_axis=0, tiled=True)  16.2 us
    all_to_all x1, starting transfers between devices, per_device(): lax.all_to_all(lax.all_to_all(pick_rows(weighted, slot_wave), 'band', spl...  15.5 us
    gather x4, local copies, waits for them, and re-layouts, pick_rows(): return flat[order].reshape(weighted.shape)  10.2 us
    all_to_all x2, local copies, waits for them, and re-layouts, per_device(): lax.all_to_all(pick_rows(weighted, slot_wave), 'band', split_axis=0, conc...  7.53 us
  transfers between devices with their start and end apart: 2, of which 2 were waited for; matrix products, arithmetic and copies ran while one was open for 3% of the time, Pallas kernels for 0%

commit v1 on v0

v1 whole, which is shorter than its diff:
```python
import functools

import jax
import jax.numpy as jnp
from jax import lax
from jax.experimental import pallas as pl
from jax.experimental.pallas import tpu as pltpu
from jax.sharding import PartitionSpec as P

MESH = pl.DeviceIdType.MESH
F32, BF16 = jnp.float32, jnp.bfloat16
LEV = 96
NX, NY, NZ = 4, 8, 12
NB, NF = NX * NY, 2 * NZ
HB = NB // 2
LATS = 56
PAIR = 2 * LATS
TAIL = 128 - PAIR
ND = HB // 2 - 1
Z_ORDER = (6, 5, -5, 4, -4, 3, -3, 2, -2, 1, -1, 0)
Y_ORDER = (4, 3, -3, 2, -2, 1, -1, 0)


def band_of(parity, j):
    return (parity + 2 * (j // NY)) * NY + j % NY


def lanes():
    return lax.broadcasted_iota(jnp.int32, (8, 128), 1)


def roll(v, by):
    return pltpu.roll(v, by % 128, 1)


def dense_to_pair(src, dst, z):
    lane = lanes()
    low = lane < LATS
    halves = []
    for core in range(2):
        f = 2 * z + core
        tiles = [src[f, i].astype(F32) for i in range(ND)]
        last = roll(tiles[0], TAIL)
        for i in range(1, ND):
            last = jnp.where(lane < TAIL * i, last, roll(tiles[i], TAIL + TAIL * i))
        halves.append(tiles + [last])
    for i in range(ND + 1):
        one, two = halves[0][i], halves[1][i]
        dst[2 * i, z] = jnp.where(low, one, roll(two, LATS)).astype(BF16)
        dst[2 * i + 1, z] = jnp.where(low, roll(one, -LATS), two).astype(BF16)


def pair_to_dense(src, z):
    lane = lanes()
    low, body = lane < LATS, lane < PAIR
    first, second = [], []
    for i in range(ND + 1):
        even, odd = src[2 * i, z].astype(F32), src[2 * i + 1, z].astype(F32)
        first.append(jnp.where(low, even, roll(odd, LATS)))
        second.append(jnp.where(low, roll(even, -LATS), odd))
    out = []
    for tiles in (first, second):
        out.append([jnp.where(body, tiles[i], roll(tiles[ND], PAIR - TAIL * i)) for i in range(ND)])
    return out


def exchange_kernel(
    waves, quad, rates, proj, recon, fourier_hbm, legendre_hbm,
    spectral, last_a, last_b,
    fourier, legendre, left, direct,
    sa1, ra1, sa2, ra2, sb1, rb1, sb2, rb2,
    xa, ya, za, xb, yb, zb, vb,
    local_sem, send_sem, recv_sem,
):
    b, f = lax.axis_index("band"), lax.axis_index("field")
    x, y = b // NY, lax.rem(b, NY)
    z, core = f // 2, lax.rem(f, 2)
    parity, mine = lax.rem(x, 2), (x // 2) * NY + y

    barrier = pltpu.get_barrier_semaphore()

    def greet_band(i, carry):
        pl.semaphore_signal(barrier, 1, device_id=(lax.rem(b + i, NB), f), device_id_type=MESH)
        return carry

    def greet_field(i, carry):
        pl.semaphore_signal(barrier, 1, device_id=(b, lax.rem(f + i, NF)), device_id_type=MESH)
        return carry

    lax.fori_loop(1, NF, greet_field, 0)
    lax.fori_loop(1, NB, greet_band, 0)

    fetch = pltpu.make_async_copy(fourier_hbm, fourier, local_sem.at[0])
    fetch.start()
    table = []
    for part in range(2):
        side = parity if part == 0 else 1 - parity
        tail_at = band_of(side, HB - 2) * LATS
        for i in range(ND):
            row = (part * ND + i) * 128
            at = pl.multiple_of(band_of(side, 2 * i) * LATS, 16)
            table.append(pltpu.make_async_copy(
                legendre_hbm.at[0, pl.ds(at, PAIR)], legendre.at[pl.ds(row, PAIR)], local_sem.at[1]))
            at = pl.multiple_of(tail_at + TAIL * i, 16)
            table.append(pltpu.make_async_copy(
                legendre_hbm.at[0, pl.ds(at, TAIL)], legendre.at[pl.ds(row + PAIR, TAIL)], local_sem.at[1]))
    for copy in table:
        copy.start()
    fetch.wait()

    weight = quad[...]

    def picked(band, field):
        wave = waves[band * NF + field]
        return fourier[wave].astype(F32) * weight

    def pack_dense(field, carry):
        pieces = [picked(band_of(parity, j), field) for j in range(HB)]
        last = jnp.concatenate(pieces[HB - 2:], axis=1)
        for i in range(ND):
            tail = last[:, TAIL * i:TAIL * (i + 1)]
            tile = jnp.concatenate([pieces[2 * i], pieces[2 * i + 1], tail], axis=1)
            sa1[field, i] = tile.astype(BF16)
        return carry

    lax.fori_loop(0, NF, pack_dense, 0)
    empty = jnp.zeros((8, TAIL), F32)

    def pack_pair(j, carry):
        band = (1 - parity + 2 * (j // NY)) * NY + lax.rem(j, NY)
        for k in range(NZ):
            tile = jnp.concatenate([picked(band, 2 * k), picked(band, 2 * k + 1), empty], axis=1)
            sb1[j, k] = tile.astype(BF16)
        return carry

    lax.fori_loop(0, HB, pack_pair, 0)
    pl.semaphore_wait(barrier, NB + NF - 2)

    def send(src, dst, phase, device):
        pltpu.make_async_remote_copy(
            src_ref=src, dst_ref=dst, send_sem=send_sem.at[phase], recv_sem=recv_sem.at[phase],
            device_id=device, device_id_type=MESH).start()

    def send_field(src, dst, phase):
        for d in Z_ORDER:
            for k in range(2):
                if d == 0 and k == 0:
                    continue
                to = lax.rem(z + d + NZ, NZ) * 2 + lax.rem(core + k, 2)
                send(src.at[to], dst.at[f], phase, (b, to))

    def send_band(src, dst, phase, same):
        steps = (2, 0) if same else (1, 3)
        for dy in Y_ORDER:
            for dx in steps:
                if dx == 0 and dy == 0:
                    continue
                to_x, to_y = lax.rem(x + dx, NX), lax.rem(y + dy + NY, NY)
                to = (to_x // 2) * NY + to_y
                send(src.at[to], dst.at[mine], phase, (to_x * NY + to_y, f))

    def wait_all(ref, phase, count, received):
        some = ref.at[pl.ds(0, count)]
        copy = pltpu.make_async_remote_copy(
            src_ref=some, dst_ref=some, send_sem=send_sem.at[phase], recv_sem=recv_sem.at[phase],
            device_id=(b, f), device_id_type=MESH)
        if received:
            copy.wait_recv()
        else:
            copy.wait_send()

    def over_z(body):
        def step(k, carry):
            body(k)
            return carry

        lax.fori_loop(0, NZ, step, 0)

    def put_dense(src, dst):
        def body(k):
            out = pair_to_dense(src, k)
            for c in range(2):
                for i in range(ND):
                    dst[2 * k + c, i] = out[c][i].astype(BF16)

        over_z(body)

    send_field(sa1, ra1, 0)
    send_band(sb1, rb1, 1, False)
    ra1[f] = sa1[f]

    wait_all(rb1, 1, HB, True)
    put_dense(rb1, sb2)
    send_field(sb2, rb2, 2)
    rb2[f] = sb2[f]

    wait_all(ra1, 0, NF - 1, True)
    over_z(functools.partial(dense_to_pair, ra1, sa2))
    send_band(sa2, ra2, 3, True)
    ra2[mine] = sa2[mine]

    for copy in table:
        copy.wait()
    total = spectral.shape[1]
    step_n = 256
    half_k = ND * 128

    wait_all(ra2, 3, HB - 1, True)

    def left_a(k):
        out = pair_to_dense(ra2, k)
        for i in range(ND):
            both = jnp.concatenate([out[0][i], out[1][i]], axis=0)
            left[pl.ds(pl.multiple_of(16 * k, 16), 16), 128 * i:128 * (i + 1)] = both.astype(BF16)

    over_z(left_a)
    for n in range(0, total, step_n):
        direct[:, n:n + step_n] = jnp.dot(
            left[:, :half_k], legendre[:half_k, n:n + step_n], preferred_element_type=F32)

    wait_all(rb2, 2, NF - 1, True)

    def left_b(k):
        for i in range(ND):
            both = jnp.concatenate([rb2[2 * k, i].astype(F32), rb2[2 * k + 1, i].astype(F32)], axis=0)
            left[pl.ds(pl.multiple_of(16 * k, 16), 16), half_k + 128 * i:half_k + 128 * (i + 1)] = both.astype(BF16)

    over_z(left_b)
    my_wave = waves[b * NF + f]
    for n in range(0, total, step_n):
        part = direct[:, n:n + step_n] + jnp.dot(
            left[:, half_k:], legendre[half_k:, n:n + step_n], preferred_element_type=F32)
        order = (lax.broadcasted_iota(jnp.int32, (LEV, step_n), 1) + n).astype(F32)
        gamma = 1.0 / (1.0 + rates[...] * (order * (order + 1.0) / float(total * total)))
        degree = lax.broadcasted_iota(jnp.int32, (LEV, step_n), 1) + n
        for c in range(2):
            modes = gamma * jnp.dot(
                proj[...], part[LEV * c:LEV * (c + 1)], precision=lax.Precision.HIGHEST, preferred_element_type=F32)
            solved = jnp.dot(recon[...], modes, precision=lax.Precision.HIGHEST, preferred_element_type=F32)
            kept = jnp.where(degree >= my_wave, solved, 0.0)
            spectral[LEV * c:LEV * (c + 1), n:n + step_n] = kept.astype(BF16)

    def back(part, out):
        for i in range(ND):
            row = (part * ND + i) * 128
            made = lax.dot_general(
                spectral[...], legendre[row:row + 128, :], (((1,), (1,)), ((), ())), preferred_element_type=F32)
            out[:, i] = made.reshape(NF, 8, 128).astype(BF16)

    back(0, xa)
    send_field(xa, ya, 4)
    ya[f] = xa[f]
    back(1, xb)
    over_z(functools.partial(dense_to_pair, xb, yb))
    send_band(yb, zb, 5, False)

    wait_all(zb, 5, HB, True)
    put_dense(zb, vb)
    send_field(vb, last_b, 6)
    last_b[f] = vb[f]

    wait_all(ya, 4, NF - 1, True)
    over_z(functools.partial(dense_to_pair, ya, za))
    send_band(za, last_a, 7, True)
    last_a[mine] = za[mine]

    wait_all(last_a, 7, HB - 1, True)
    wait_all(last_b, 6, NF - 1, True)
    for ref, phase, count in (
        (sa1, 0, NF - 1), (sb1, 1, HB), (sb2, 2, NF - 1), (sa2, 3, HB - 1),
        (xa, 4, NF - 1), (yb, 5, HB), (vb, 6, NF - 1), (za, 7, HB - 1),
    ):
        wait_all(ref, phase, count, False)


def place_kernel(waves, from_a, from_b, returned):
    b = lax.axis_index("band")
    parity = lax.rem(b // NY, 2)
    lane = lanes()

    def put(band, field, tile):
        returned[waves[band * NF + field]] = tile[:, :LATS].astype(BF16)

    def one_a(j, carry):
        band = (parity + 2 * (j // NY)) * NY + lax.rem(j, NY)
        for k in range(NZ):
            tile = from_a[j, k].astype(F32)
            put(band, 2 * k, tile)
            put(band, 2 * k + 1, roll(tile, -LATS))
        return carry

    lax.fori_loop(0, HB, one_a, 0)

    def one_b(field, carry):
        tiles = [from_b[field, i].astype(F32) for i in range(ND)]
        last = roll(tiles[0], TAIL)
        for i in range(1, ND):
            last = jnp.where(lane < TAIL * i, last, roll(tiles[i], TAIL + TAIL * i))
        for i, tile in enumerate(tiles + [last]):
            put(band_of(1 - parity, 2 * i), field, tile)
            put(band_of(1 - parity, 2 * i + 1), field, roll(tile, -LATS))
        return carry

    lax.fori_loop(0, NF, one_b, 0)


def per_device(fourier, quad_weights, legendre, slot_wave, vert_proj, vert_recon, vert_rates):
    nlat, total = legendre.shape[1:]
    dense = (NF, ND, 8, 128)
    pair = (HB, NZ, 8, 128)
    vmem, smem = pl.BlockSpec(memory_space=pltpu.VMEM), pl.BlockSpec(memory_space=pltpu.SMEM)
    anywhere = pl.BlockSpec(memory_space=pl.ANY)
    buffers = [dense, dense, pair, pair, pair, pair, dense, dense, dense, dense, pair, dense, pair, pair, dense]
    spectral, last_a, last_b = pl.pallas_call(
        exchange_kernel,
        out_shape=(
            jax.ShapeDtypeStruct((2 * LEV, total), BF16),
            jax.ShapeDtypeStruct(pair, BF16),
            jax.ShapeDtypeStruct(dense, BF16),
        ),
        in_specs=[smem, vmem, vmem, vmem, vmem, anywhere, anywhere],
        out_specs=[vmem, vmem, vmem],
        scratch_shapes=[
            pltpu.VMEM(fourier.shape, BF16),
            pltpu.VMEM((nlat, total), BF16),
            pltpu.VMEM((2 * LEV, nlat), BF16),
            pltpu.VMEM((2 * LEV, total), F32),
        ]
        + [pltpu.VMEM(shape, BF16) for shape in buffers]
        + [pltpu.SemaphoreType.DMA((2,)), pltpu.SemaphoreType.DMA((8,)), pltpu.SemaphoreType.DMA((8,))],
        compiler_params=pltpu.CompilerParams(
            collective_id=0, has_side_effects=True, vmem_limit_bytes=48 * 1024 * 1024),
        name="exchange",
    )(slot_wave, quad_weights.reshape(1, LATS), vert_rates.reshape(LEV, 1), vert_proj, vert_recon, fourier, legendre)
    returned = pl.pallas_call(
        place_kernel,
        out_shape=jax.ShapeDtypeStruct(fourier.shape, BF16),
        in_specs=[smem, vmem, vmem],
        out_specs=vmem,
        name="place",
    )(slot_wave, last_a, last_b)
    return spectral.reshape(1, 2, LEV, total), returned


def solution(mesh):
    placed = (
        P(None, "field", "band"),
        P("band"),
        P(("band", "field"), None, None),
        P(),
        P(),
        P(),
        P(),
    )
    return jax.shard_map(
        per_device,
        mesh=mesh,
        in_specs=placed,
        out_specs=(P(("band", "field"), None, None, None), P(None, "field", "band")),
        check_vma=False,
    )
```

time: 211 us -> 103 us (0.49)
  the two profiles are of different devices: /device:TPU:8 before, /device:TPU:1 now
where the time goes in v1:
time: 103 us
  Pallas kernels  92.8 us (90%)
  local copies, waits for them, and re-layouts  9.44 us (9%)
    pallas_call x1, Pallas kernels, per_device(): pl.pallas_call(exchange_kernel, out_shape=(jax.ShapeDtypeStruct((2 * LEV,...  85.7 us
    unnamed x17, local copies, waits for them, and re-layouts  8.65 us
    pallas_call x1, Pallas kernels, per_device(): pl.pallas_call(place_kernel, out_shape=jax.ShapeDtypeStruct(fourier.shape...  7.13 us

profile of v1, /device:TPU:1, one launch (start us, length us, event | category | flops | bytes accessed | tf_op | source)
XLA Modules:
  0.0 103.0 jit_solution(11181724537837799574)
XLA Ops:
  0.6 0.0 copy-start.5
  0.6 0.0 copy-start.4
  0.7 0.0 copy-start.3
  0.7 0.0 copy-start.6
  0.7 0.8 copy.9.rates
  1.5 2.0 %copy.10.fourier_hbm = bf16[768,8,56]{2,1,0:T(8,128)(2,1)S(1)} copy(bf16[768,8,56]{0,2,1:T(8,128)(2,1)} %param.7) | data formatting | bytes 1376256 | tf_op args[0]
  3.5 0.0 copy-done.5
  3.5 0.0 copy-done.4
  3.5 0.0 copy-done.3
  3.5 0.0 copy-done.6
  3.5 0.0 copy-start
  3.5 1.8 %copy-done = bf16[1,1792,768]{2,1,0:T(8,128)(2,1)S(1)} copy-done((bf16[1,1792,768]{2,1,0:T(8,128)(2,1)S(1)}, bf16[1,1792,768]{2,1,0:T(8,128)(2,1)}, u32[]{:S(2)}) %copy-start) | copy-done | bytes 2752536
  5.3 85.7 %exchange.1 = (bf16[192,768]{1,0:T(8,128)(2,1)S(1)}, bf16[16,12,8,128]{3,2,1,0:T(8,128)(2,1)S(1)}, bf16[24,7,8,128]{3,2,1,0:T(8,128)(2,1)S(1)}) custom-call(s32[768]{0:T(1024)S(1)} %copy-done.5, f32[1,56]{1,0:T(1,128)S(1)} %bitcast.4, f32[96,1]{1,0:T(8,128)S(1)} %copy.9.rates, f32[96,96]{1,0:T(8,128)S(1)} %copy-done.3, f32[96,96]{1,0:T(8,128)S(1)} %copy-done.4, ...), custom_call_target="tpu_custom_call" | custom-call | tf_op jit(solution)/shard_map/exchange/pallas_call | solution.py:314
  91.0 0.0 copy-start.1
  91.0 0.7 copy-done.1
  91.7 0.0 copy-start.2
  91.7 0.7 copy-done.2
  92.5 7.1 %place.1 = bf16[768,8,56]{2,1,0:T(8,128)(2,1)} custom-call(s32[768]{0:T(1024)} %waves.3, bf16[16,12,8,128]{3,2,1,0:T(8,128)(2,1)} %copy-done.1, bf16[24,7,8,128]{3,2,1,0:T(8,128)(2,1)} %copy-done.2), custom_call_target="tpu_custom_call" | custom-call | tf_op jit(solution)/shard_map/place/pallas_call | solution.py:335
  99.6 2.7 %copy.11 = bf16[768,8,56]{0,2,1:T(8,128)(2,1)} copy(bf16[768,8,56]{2,1,0:T(8,128)(2,1)} %place.1) | data formatting | bytes 1376256
  102.3 0.7 copy.13
Async XLA Ops:
  0.6 2.8 %copy-start.5 = (s32[768]{0:T(1024)S(1)}, s32[768]{0:T(1024)}, u32[]{:S(2)}) copy-start(s32[768]{0:T(1024)} %waves.3) | copy-start | bytes 9220
  0.6 2.8 %copy-start.4 = (f32[96,96]{1,0:T(8,128)S(1)}, f32[96,96]{1,0:T(8,128)}, u32[]{:S(2)}) copy-start(f32[96,96]{1,0:T(8,128)} %recon.1) | copy-start | bytes 110596
  0.7 2.8 %copy-start.3 = (f32[96,96]{1,0:T(8,128)S(1)}, f32[96,96]{1,0:T(8,128)}, u32[]{:S(2)}) copy-start(f32[96,96]{1,0:T(8,128)} %proj.1) | copy-start | bytes 110596
  0.7 2.8 %copy-start.6 = (f32[56]{0:T(128)S(1)}, f32[56]{0:T(128)}, u32[]{:S(2)}) copy-start(f32[56]{0:T(128)} %param.8) | copy-start | bytes 676
  3.5 1.8 %copy-start = (bf16[1,1792,768]{2,1,0:T(8,128)(2,1)S(1)}, bf16[1,1792,768]{2,1,0:T(8,128)(2,1)}, u32[]{:S(2)}) copy-start(bf16[1,1792,768]{2,1,0:T(8,128)(2,1)} %legendre_hbm.1) | copy-start | bytes 8257540
  91.0 0.7 copy-start.1
  91.7 0.7 copy-start.2

commit v2 on v1

--- a/solution.py
+++ b/solution.py
@@ -64,10 +64,21 @@
     return out
 
 
+def parts_of(v):
+    high = v.astype(BF16)
+    return high, (v - high.astype(F32)).astype(BF16)
+
+
+def near_exact(left, right):
+    high, low = parts_of(right)
+    small = jnp.dot(left[0], low, preferred_element_type=F32) + jnp.dot(left[1], high, preferred_element_type=F32)
+    return jnp.dot(left[0], high, preferred_element_type=F32) + small
+
+
 def exchange_kernel(
-    waves, quad, rates, proj, recon, fourier_hbm, legendre_hbm,
+    waves, quad, rates, proj, recon, fourier, legendre_hbm,
     spectral, last_a, last_b,
-    fourier, legendre, left, direct,
+    legendre, left, direct,
     sa1, ra1, sa2, ra2, sb1, rb1, sb2, rb2,
     xa, ya, za, xb, yb, zb, vb,
     local_sem, send_sem, recv_sem,
@@ -79,19 +90,11 @@
 
     barrier = pltpu.get_barrier_semaphore()
 
-    def greet_band(i, carry):
+    for i in range(1, NF):
+        pl.semaphore_signal(barrier, 1, device_id=(b, lax.rem(f + i, NF)), device_id_type=MESH)
+    for i in range(1, NB):
         pl.semaphore_signal(barrier, 1, device_id=(lax.rem(b + i, NB), f), device_id_type=MESH)
-        return carry
-
-    def greet_field(i, carry):
-        pl.semaphore_signal(barrier, 1, device_id=(b, lax.rem(f + i, NF)), device_id_type=MESH)
-        return carry
-
-    lax.fori_loop(1, NF, greet_field, 0)
-    lax.fori_loop(1, NB, greet_band, 0)
-
-    fetch = pltpu.make_async_copy(fourier_hbm, fourier, local_sem.at[0])
-    fetch.start()
+
     table = []
     for part in range(2):
         side = parity if part == 0 else 1 - parity
@@ -100,40 +103,39 @@
             row = (part * ND + i) * 128
             at = pl.multiple_of(band_of(side, 2 * i) * LATS, 16)
             table.append(pltpu.make_async_copy(
-                legendre_hbm.at[0, pl.ds(at, PAIR)], legendre.at[pl.ds(row, PAIR)], local_sem.at[1]))
+                legendre_hbm.at[0, pl.ds(at, PAIR)], legendre.at[pl.ds(row, PAIR)], local_sem))
             at = pl.multiple_of(tail_at + TAIL * i, 16)
             table.append(pltpu.make_async_copy(
-                legendre_hbm.at[0, pl.ds(at, TAIL)], legendre.at[pl.ds(row + PAIR, TAIL)], local_sem.at[1]))
+                legendre_hbm.at[0, pl.ds(at, TAIL)], legendre.at[pl.ds(row + PAIR, TAIL)], local_sem))
     for copy in table:
         copy.start()
-    fetch.wait()
-
     weight = quad[...]
 
     def picked(band, field):
         wave = waves[band * NF + field]
         return fourier[wave].astype(F32) * weight
 
+    empty = jnp.zeros((8, TAIL), F32)
+    body_lanes = lanes() < PAIR
+
+    def joined(first, second):
+        return jnp.concatenate([first, second, empty], axis=1)
+
     def pack_dense(field, carry):
-        pieces = [picked(band_of(parity, j), field) for j in range(HB)]
-        last = jnp.concatenate(pieces[HB - 2:], axis=1)
-        for i in range(ND):
-            tail = last[:, TAIL * i:TAIL * (i + 1)]
-            tile = jnp.concatenate([pieces[2 * i], pieces[2 * i + 1], tail], axis=1)
-            sa1[field, i] = tile.astype(BF16)
+        tiles = [joined(picked(band_of(parity, 2 * i), field), picked(band_of(parity, 2 * i + 1), field))
+                 for i in range(ND + 1)]
+        for i in range(ND):
+            sa1[field, i] = jnp.where(body_lanes, tiles[i], roll(tiles[ND], PAIR - TAIL * i)).astype(BF16)
         return carry
-
-    lax.fori_loop(0, NF, pack_dense, 0)
-    empty = jnp.zeros((8, TAIL), F32)
 
     def pack_pair(j, carry):
         band = (1 - parity + 2 * (j // NY)) * NY + lax.rem(j, NY)
         for k in range(NZ):
-            tile = jnp.concatenate([picked(band, 2 * k), picked(band, 2 * k + 1), empty], axis=1)
-            sb1[j, k] = tile.astype(BF16)
+            sb1[j, k] = joined(picked(band, 2 * k), picked(band, 2 * k + 1)).astype(BF16)
         return carry
 
-    lax.fori_loop(0, HB, pack_pair, 0)
+    lax.fori_loop(0, HB, pack_pair, 0, unroll=2)
+    lax.fori_loop(0, NF, pack_dense, 0, unroll=3)
     pl.semaphore_wait(barrier, NB + NF - 2)
 
     def send(src, dst, phase, device):
@@ -174,7 +176,7 @@
             body(k)
             return carry
 
-        lax.fori_loop(0, NZ, step, 0)
+        lax.fori_loop(0, NZ, step, 0, unroll=3)
 
     def put_dense(src, dst):
         def body(k):
@@ -185,8 +187,8 @@
 
         over_z(body)
 
+    send_band(sb1, rb1, 1, False)
     send_field(sa1, ra1, 0)
-    send_band(sb1, rb1, 1, False)
     ra1[f] = sa1[f]
 
     wait_all(rb1, 1, HB, True)
@@ -226,17 +228,19 @@
             left[pl.ds(pl.multiple_of(16 * k, 16), 16), half_k + 128 * i:half_k + 128 * (i + 1)] = both.astype(BF16)
 
     over_z(left_b)
+    diagonal = lax.broadcasted_iota(jnp.int32, (LEV, LEV), 0) == lax.broadcasted_iota(jnp.int32, (LEV, LEV), 1)
+    rate = jnp.sum(jnp.where(diagonal, rates[...], 0.0), axis=1, keepdims=True)
+    proj_parts, recon_parts = parts_of(proj[...]), parts_of(recon[...])
     my_wave = waves[b * NF + f]
     for n in range(0, total, step_n):
         part = direct[:, n:n + step_n] + jnp.dot(
             left[:, half_k:], legendre[half_k:, n:n + step_n], preferred_element_type=F32)
         order = (lax.broadcasted_iota(jnp.int32, (LEV, step_n), 1) + n).astype(F32)
-        gamma = 1.0 / (1.0 + rates[...] * (order * (order + 1.0) / float(total * total)))
+        gamma = 1.0 / (1.0 + rate * (order * (order + 1.0) / float(total * total)))
         degree = lax.broadcasted_iota(jnp.int32, (LEV, step_n), 1) + n
         for c in range(2):
-            modes = gamma * jnp.dot(
-                proj[...], part[LEV * c:LEV * (c + 1)], precision=lax.Precision.HIGHEST, preferred_element_type=F32)
-            solved = jnp.dot(recon[...], modes, precision=lax.Precision.HIGHEST, preferred_element_type=F32)
+            modes = gamma * near_exact(proj_parts, part[LEV * c:LEV * (c + 1)])
+            solved = near_exact(recon_parts, modes)
             kept = jnp.where(degree >= my_wave, solved, 0.0)
             spectral[LEV * c:LEV * (c + 1), n:n + step_n] = kept.astype(BF16)
 
@@ -247,12 +251,12 @@
                 spectral[...], legendre[row:row + 128, :], (((1,), (1,)), ((), ())), preferred_element_type=F32)
             out[:, i] = made.reshape(NF, 8, 128).astype(BF16)
 
+    back(1, xb)
+    over_z(functools.partial(dense_to_pair, xb, yb))
+    send_band(yb, zb, 5, False)
     back(0, xa)
     send_field(xa, ya, 4)
     ya[f] = xa[f]
-    back(1, xb)
-    over_z(functools.partial(dense_to_pair, xb, yb))
-    send_band(yb, zb, 5, False)
 
     wait_all(zb, 5, HB, True)
     put_dense(zb, vb)
@@ -273,7 +277,8 @@
         wait_all(ref, phase, count, False)
 
 
-def place_kernel(waves, from_a, from_b, returned):
+def place_kernel(waves, from_a, from_b, solved, returned, spectral):
+    spectral[...] = solved[...]
     b = lax.axis_index("band")
     parity = lax.rem(b // NY, 2)
     lane = lanes()
@@ -289,7 +294,7 @@
             put(band, 2 * k + 1, roll(tile, -LATS))
         return carry
 
-    lax.fori_loop(0, HB, one_a, 0)
+    lax.fori_loop(0, HB, one_a, 0, unroll=4)
 
     def one_b(field, carry):
         tiles = [from_b[field, i].astype(F32) for i in range(ND)]
@@ -301,7 +306,7 @@
             put(band_of(1 - parity, 2 * i + 1), field, roll(tile, -LATS))
         return carry
 
-    lax.fori_loop(0, NF, one_b, 0)
+    lax.fori_loop(0, NF, one_b, 0, unroll=4)
 
 
 def per_device(fourier, quad_weights, legendre, slot_wave, vert_proj, vert_recon, vert_rates):
@@ -309,7 +314,7 @@
     dense = (NF, ND, 8, 128)
     pair = (HB, NZ, 8, 128)
     vmem, smem = pl.BlockSpec(memory_space=pltpu.VMEM), pl.BlockSpec(memory_space=pltpu.SMEM)
-    anywhere = pl.BlockSpec(memory_space=pl.ANY)
+    hbm = pl.BlockSpec(memory_space=pltpu.HBM)
     buffers = [dense, dense, pair, pair, pair, pair, dense, dense, dense, dense, pair, dense, pair, pair, dense]
     spectral, last_a, last_b = pl.pallas_call(
         exchange_kernel,
@@ -318,27 +323,27 @@
             jax.ShapeDtypeStruct(pair, BF16),
             jax.ShapeDtypeStruct(dense, BF16),
         ),
-        in_specs=[smem, vmem, vmem, vmem, vmem, anywhere, anywhere],
+        in_specs=[smem, vmem, vmem, vmem, vmem, vmem, hbm],
         out_specs=[vmem, vmem, vmem],
         scratch_shapes=[
-            pltpu.VMEM(fourier.shape, BF16),
             pltpu.VMEM((nlat, total), BF16),
             pltpu.VMEM((2 * LEV, nlat), BF16),
             pltpu.VMEM((2 * LEV, total), F32),
         ]
         + [pltpu.VMEM(shape, BF16) for shape in buffers]
-        + [pltpu.SemaphoreType.DMA((2,)), pltpu.SemaphoreType.DMA((8,)), pltpu.SemaphoreType.DMA((8,))],
+        + [pltpu.SemaphoreType.DMA, pltpu.SemaphoreType.DMA((8,)), pltpu.SemaphoreType.DMA((8,))],
         compiler_params=pltpu.CompilerParams(
-            collective_id=0, has_side_effects=True, vmem_limit_bytes=48 * 1024 * 1024),
+            collective_id=0, has_side_effects=True, vmem_limit_bytes=52_500_000),
         name="exchange",
-    )(slot_wave, quad_weights.reshape(1, LATS), vert_rates.reshape(LEV, 1), vert_proj, vert_recon, fourier, legendre)
-    returned = pl.pallas_call(
+    )(slot_wave, quad_weights.reshape(1, LATS), vert_rates.reshape(1, LEV), vert_proj, vert_recon, fourier, legendre)
+    returned, spectral = pl.pallas_call(
         place_kernel,
-        out_shape=jax.ShapeDtypeStruct(fourier.shape, BF16),
-        in_specs=[smem, vmem, vmem],
-        out_specs=vmem,
+        out_shape=(jax.ShapeDtypeStruct(fourier.shape, BF16), jax.ShapeDtypeStruct(spectral.shape, BF16)),
+        in_specs=[smem, vmem, vmem, vmem],
+        out_specs=[vmem, vmem],
+        compiler_params=pltpu.CompilerParams(vmem_limit_bytes=16 * 1024 * 1024),
         name="place",
-    )(slot_wave, last_a, last_b)
+    )(slot_wave, last_a, last_b, spectral)
     return spectral.reshape(1, 2, LEV, total), returned
 
 

time: 103 us -> 85.8 us (0.83)
  Pallas kernels: 92.8 us -> 81.2 us
  local copies, waits for them, and re-layouts: 9.44 us -> 3.72 us
    pallas_call x1, Pallas kernels: 85.7 us -> 78.1 us  [per_device(): pl.pallas_call(exchange_kernel, out_shape=(jax.ShapeDtypeStruct((2 * LEV,...]
    unnamed x17 -> x12, local copies, waits for them, and re-layouts: 8.65 us -> 3.72 us
    pallas_call x1, Pallas kernels: 7.13 us -> 3.11 us  [per_device(): pl.pallas_call(place_kernel, out_shape=(jax.ShapeDtypeStruct(fourier.shap...]
where the time goes in v2:
time: 85.8 us; the launch traced here: 85.7 us
  Pallas kernels  81.2 us (95%)
  local copies, waits for them, and re-layouts  3.72 us (4%)
    pallas_call x1, Pallas kernels, per_device(): pl.pallas_call(exchange_kernel, out_shape=(jax.ShapeDtypeStruct((2 * LEV,...  78.1 us
    unnamed x12, local copies, waits for them, and re-layouts  3.72 us
    pallas_call x1, Pallas kernels, per_device(): pl.pallas_call(place_kernel, out_shape=(jax.ShapeDtypeStruct(fourier.shap...  3.11 us

profile of v2, /device:TPU:1, one launch (start us, length us, event | category | flops | bytes accessed | tf_op | source)
XLA Modules:
  0.0 85.7 jit_solution(8973474422546718754)
XLA Ops:
  0.6 0.0 copy-start.2
  0.6 0.0 copy-start.4
  0.7 0.0 copy-start.1
  0.7 0.0 copy-start
  0.7 0.0 copy-start.3
  0.7 2.0 %copy.9.fourier = bf16[768,8,56]{2,1,0:T(8,128)(2,1)S(1)} copy(bf16[768,8,56]{0,2,1:T(8,128)(2,1)} %param.7) | data formatting | bytes 1376256 | tf_op args[0]
  2.7 0.0 copy-done.2
  2.7 0.0 copy-done.4
  2.7 0.0 copy-done.1
  2.8 0.0 copy-done
  2.8 0.0 copy-done.3
  2.8 78.1 %exchange.1 = (bf16[192,768]{1,0:T(8,128)(2,1)S(1)}, bf16[16,12,8,128]{3,2,1,0:T(8,128)(2,1)S(1)}, bf16[24,7,8,128]{3,2,1,0:T(8,128)(2,1)S(1)}) custom-call(s32[768]{0:T(1024)S(1)} %copy-done.2, f32[1,56]{1,0:T(1,128)S(1)} %bitcast.3, f32[1,96]{1,0:T(1,128)S(1)} %bitcast.4, f32[96,96]{1,0:T(8,128)S(1)} %copy-done, f32[96,96]{1,0:T(8,128)S(1)} %copy-done.1, ...), custom_call_target="tpu_custom_call" | custom-call | tf_op jit(solution)/shard_map/exchange/pallas_call | solution.py:319
  80.9 3.1 %place.1 = (bf16[768,8,56]{2,1,0:T(8,128)(2,1)S(1)}, bf16[192,768]{1,0:T(8,128)(2,1)}) custom-call(s32[768]{0:T(1024)S(1)} %copy-done.2, bf16[16,12,8,128]{3,2,1,0:T(8,128)(2,1)S(1)} %get-tuple-element.7.from_a, bf16[24,7,8,128]{3,2,1,0:T(8,128)(2,1)S(1)} %get-tuple-element.8.from_b, bf16[192,768]{1,0:T(8,128)(2,1)S(1)} %get-tuple-element.9.solved), custom_call_target="tpu_custom_call" | custom-call | tf_op jit(solution)/shard_map/place/pallas_call | solution.py:339
  84.0 1.7 %copy.10 = bf16[768,8,56]{0,2,1:T(8,128)(2,1)} copy(bf16[768,8,56]{2,1,0:T(8,128)(2,1)S(1)} %get-tuple-element.13) | data formatting | bytes 1376256
Async XLA Ops:
  0.6 2.1 %copy-start.2 = (s32[768]{0:T(1024)S(1)}, s32[768]{0:T(1024)}, u32[]{:S(2)}) copy-start(s32[768]{0:T(1024)} %waves.3) | copy-start | bytes 9220
  0.6 2.1 %copy-start.4 = (f32[96]{0:T(128)S(1)}, f32[96]{0:T(128)}, u32[]{:S(2)}) copy-start(f32[96]{0:T(128)} %param.13) | copy-start | bytes 1156
  0.7 2.1 %copy-start.1 = (f32[96,96]{1,0:T(8,128)S(1)}, f32[96,96]{1,0:T(8,128)}, u32[]{:S(2)}) copy-start(f32[96,96]{1,0:T(8,128)} %recon.1) | copy-start | bytes 110596
  0.7 2.1 %copy-start = (f32[96,96]{1,0:T(8,128)S(1)}, f32[96,96]{1,0:T(8,128)}, u32[]{:S(2)}) copy-start(f32[96,96]{1,0:T(8,128)} %proj.1) | copy-start | bytes 110596
  0.7 2.1 %copy-start.3 = (f32[56]{0:T(128)S(1)}, f32[56]{0:T(128)}, u32[]{:S(2)}) copy-start(f32[56]{0:T(128)} %param.8) | copy-start | bytes 676

commit v3 on v2

--- a/solution.py
+++ b/solution.py
@@ -17,6 +17,7 @@
 PAIR = 2 * LATS
 TAIL = 128 - PAIR
 ND = HB // 2 - 1
+SKEW = 8 * (ND + 1) + 8
 Z_ORDER = (6, 5, -5, 4, -4, 3, -3, 2, -2, 1, -1, 0)
 Y_ORDER = (4, 3, -3, 2, -2, 1, -1, 0)
 
@@ -64,6 +65,12 @@
     return out
 
 
+def turned(row):
+    n = row.shape[1]
+    diagonal = lax.broadcasted_iota(jnp.int32, (n, n), 0) == lax.broadcasted_iota(jnp.int32, (n, n), 1)
+    return jnp.sum(jnp.where(diagonal, row, 0.0), axis=1, keepdims=True)
+
+
 def parts_of(v):
     high = v.astype(BF16)
     return high, (v - high.astype(F32)).astype(BF16)
@@ -76,12 +83,12 @@
 
 
 def exchange_kernel(
-    waves, quad, rates, proj, recon, fourier, legendre_hbm,
+    waves_hbm, quad_hbm, rates_hbm, proj_hbm, recon_hbm, fourier_hbm, legendre_hbm,
     spectral, last_a, last_b,
-    legendre, left, direct,
+    waves, quad, rates, proj, recon, legendre, left, direct, fourier, weighted, chosen, gathered, tiles_a, tiles_b,
     sa1, ra1, sa2, ra2, sb1, rb1, sb2, rb2,
     xa, ya, za, xb, yb, zb, vb,
-    local_sem, send_sem, recv_sem,
+    small_sem, local_sem, fetch_sem, send_sem, recv_sem,
 ):
     b, f = lax.axis_index("band"), lax.axis_index("field")
     x, y = b // NY, lax.rem(b, NY)
@@ -89,6 +96,15 @@
     parity, mine = lax.rem(x, 2), (x // 2) * NY + y
 
     barrier = pltpu.get_barrier_semaphore()
+
+    small = [
+        pltpu.make_async_copy(src, dst, small_sem.at[i])
+        for i, (src, dst) in enumerate(
+            ((waves_hbm, waves), (quad_hbm, quad), (rates_hbm, rates), (proj_hbm, proj), (recon_hbm, recon)))]
+    fetch = pltpu.make_async_copy(fourier_hbm, fourier, fetch_sem)
+    for copy in small:
+        copy.start()
+    fetch.start()
 
     for i in range(1, NF):
         pl.semaphore_signal(barrier, 1, device_id=(b, lax.rem(f + i, NF)), device_id_type=MESH)
@@ -109,32 +125,64 @@
                 legendre_hbm.at[0, pl.ds(at, TAIL)], legendre.at[pl.ds(row + PAIR, TAIL)], local_sem))
     for copy in table:
         copy.start()
-    weight = quad[...]
-
-    def picked(band, field):
-        wave = waves[band * NF + field]
-        return fourier[wave].astype(F32) * weight
-
-    empty = jnp.zeros((8, TAIL), F32)
-    body_lanes = lanes() < PAIR
-
-    def joined(first, second):
-        return jnp.concatenate([first, second, empty], axis=1)
+    for copy in small:
+        copy.wait()
+    total = spectral.shape[1]
+    wave_of_lane = lax.broadcasted_iota(jnp.int32, (128, total), 1).astype(F32)
+    for t in range(total // 128):
+        column = turned(waves[t:t + 1, :].astype(F32))
+        chosen[128 * t:128 * (t + 1)] = jnp.where(wave_of_lane == column, 1.0, 0.0).astype(BF16)
+    weight = turned(quad[...])
+    fetch.wait()
+    for r in range(8):
+        rows = jnp.concatenate([fourier[r].astype(F32) * weight, jnp.zeros((8, total), F32)], axis=0)
+        weighted[64 * r:64 * (r + 1)] = rows.astype(BF16)
+    for n in range(2):
+        found = lax.dot_general(
+            chosen[...], weighted[256 * n:256 * (n + 1)], (((1,), (1,)), ((), ())), preferred_element_type=F32)
+        gathered[2 * n] = found[:, :128]
+        gathered[2 * n + 1] = found[:, 128:]
+
+    low_lanes, body_lanes = lanes() < LATS, lanes() < PAIR
+
+    def side_by_side(even, odd, r):
+        if r % 2 == 0:
+            return jnp.where(low_lanes, even, roll(odd, LATS))
+        return jnp.where(low_lanes, roll(even, -64), roll(odd, LATS - 64))
+
+    def rows_pair(t, carry):
+        for half in range(2):
+            start = (1 - parity + 2 * half) * NY * NF + 16 * t
+            for r in range(8):
+                even = gathered[r // 2, pl.ds(start, 8, stride=2), :]
+                odd = gathered[r // 2, pl.ds(start + 1, 8, stride=2), :]
+                at = (half * NY * NZ + 8 * t) * 8 + r
+                tiles_b[pl.ds(at, 8, stride=8), :] = side_by_side(even, odd, r)
+        return carry
+
+    def rows_dense(i, carry):
+        band = (parity + 2 * ((2 * i) // NY)) * NY + lax.rem(2 * i, NY)
+        for t in range(NF // 8):
+            start = pl.multiple_of(band * NF + 8 * t, 8)
+            for r in range(8):
+                even = gathered[r // 2, pl.ds(start, 8), :]
+                odd = gathered[r // 2, pl.ds(pl.multiple_of(start + NF, 8), 8), :]
+                at = 8 * t * SKEW + 8 * i + r
+                tiles_a[pl.ds(at, 8, stride=SKEW), :] = side_by_side(even, odd, r)
+        return carry
+
+    def pack_pair(j, carry):
+        for k in range(NZ):
+            sb1[j, k] = tiles_b[pl.ds(pl.multiple_of((j * NZ + k) * 8, 8), 8), :].astype(BF16)
+        return carry
 
     def pack_dense(field, carry):
-        tiles = [joined(picked(band_of(parity, 2 * i), field), picked(band_of(parity, 2 * i + 1), field))
-                 for i in range(ND + 1)]
+        tiles = [tiles_a[pl.ds(pl.multiple_of(field * SKEW + 8 * i, 8), 8), :] for i in range(ND + 1)]
         for i in range(ND):
             sa1[field, i] = jnp.where(body_lanes, tiles[i], roll(tiles[ND], PAIR - TAIL * i)).astype(BF16)
         return carry
 
-    def pack_pair(j, carry):
-        band = (1 - parity + 2 * (j // NY)) * NY + lax.rem(j, NY)
-        for k in range(NZ):
-            sb1[j, k] = joined(picked(band, 2 * k), picked(band, 2 * k + 1)).astype(BF16)
-        return carry
-
-    lax.fori_loop(0, HB, pack_pair, 0, unroll=2)
+    lax.fori_loop(0, ND + 1, rows_dense, 0, unroll=2)
     lax.fori_loop(0, NF, pack_dense, 0, unroll=3)
     pl.semaphore_wait(barrier, NB + NF - 2)
 
@@ -187,8 +235,10 @@
 
         over_z(body)
 
+    send_field(sa1, ra1, 0)
+    lax.fori_loop(0, NY * NZ // 8, rows_pair, 0, unroll=2)
+    lax.fori_loop(0, HB, pack_pair, 0, unroll=2)
     send_band(sb1, rb1, 1, False)
-    send_field(sa1, ra1, 0)
     ra1[f] = sa1[f]
 
     wait_all(rb1, 1, HB, True)
@@ -203,7 +253,6 @@
 
     for copy in table:
         copy.wait()
-    total = spectral.shape[1]
     step_n = 256
     half_k = ND * 128
 
@@ -228,20 +277,20 @@
             left[pl.ds(pl.multiple_of(16 * k, 16), 16), half_k + 128 * i:half_k + 128 * (i + 1)] = both.astype(BF16)
 
     over_z(left_b)
-    diagonal = lax.broadcasted_iota(jnp.int32, (LEV, LEV), 0) == lax.broadcasted_iota(jnp.int32, (LEV, LEV), 1)
-    rate = jnp.sum(jnp.where(diagonal, rates[...], 0.0), axis=1, keepdims=True)
+    rate = turned(rates[...])
     proj_parts, recon_parts = parts_of(proj[...]), parts_of(recon[...])
-    my_wave = waves[b * NF + f]
+    place_of = lax.broadcasted_iota(jnp.int32, waves.shape, 0) * 128 + lax.broadcasted_iota(jnp.int32, waves.shape, 1)
+    mine_only = jnp.where(place_of == b * NF + f, waves[...].astype(F32), 0.0)
+    my_wave = jnp.sum(jnp.sum(mine_only, axis=1, keepdims=True), axis=0, keepdims=True)
     for n in range(0, total, step_n):
         part = direct[:, n:n + step_n] + jnp.dot(
             left[:, half_k:], legendre[half_k:, n:n + step_n], preferred_element_type=F32)
         order = (lax.broadcasted_iota(jnp.int32, (LEV, step_n), 1) + n).astype(F32)
         gamma = 1.0 / (1.0 + rate * (order * (order + 1.0) / float(total * total)))
-        degree = lax.broadcasted_iota(jnp.int32, (LEV, step_n), 1) + n
         for c in range(2):
             modes = gamma * near_exact(proj_parts, part[LEV * c:LEV * (c + 1)])
             solved = near_exact(recon_parts, modes)
-            kept = jnp.where(degree >= my_wave, solved, 0.0)
+            kept = jnp.where(order >= my_wave, solved, 0.0)
             spectral[LEV * c:LEV * (c + 1), n:n + step_n] = kept.astype(BF16)
 
     def back(part, out):
@@ -323,19 +372,32 @@
             jax.ShapeDtypeStruct(pair, BF16),
             jax.ShapeDtypeStruct(dense, BF16),
         ),
-        in_specs=[smem, vmem, vmem, vmem, vmem, vmem, hbm],
+        in_specs=[hbm] * 7,
         out_specs=[vmem, vmem, vmem],
         scratch_shapes=[
+            pltpu.VMEM((total // 128, 128), jnp.int32),
+            pltpu.VMEM((1, LATS), F32),
+            pltpu.VMEM((1, LEV), F32),
+            pltpu.VMEM((LEV, LEV), F32),
+            pltpu.VMEM((LEV, LEV), F32),
             pltpu.VMEM((nlat, total), BF16),
             pltpu.VMEM((2 * LEV, nlat), BF16),
             pltpu.VMEM((2 * LEV, total), F32),
+            pltpu.VMEM((8, LATS, total), BF16),
+            pltpu.VMEM((512, total), BF16),
+            pltpu.VMEM((total, total), BF16),
+            pltpu.VMEM((4, total, 128), F32),
+            pltpu.VMEM((NF * SKEW, 128), F32),
+            pltpu.VMEM((HB * NZ * 8, 128), F32),
         ]
         + [pltpu.VMEM(shape, BF16) for shape in buffers]
-        + [pltpu.SemaphoreType.DMA, pltpu.SemaphoreType.DMA((8,)), pltpu.SemaphoreType.DMA((8,))],
+        + [pltpu.SemaphoreType.DMA((5,)), pltpu.SemaphoreType.DMA, pltpu.SemaphoreType.DMA, pltpu.SemaphoreType.DMA((8,)), pltpu.SemaphoreType.DMA((8,))],
         compiler_params=pltpu.CompilerParams(
-            collective_id=0, has_side_effects=True, vmem_limit_bytes=52_500_000),
+            collective_id=0, has_side_effects=True, vmem_limit_bytes=55_000_000),
         name="exchange",
-    )(slot_wave, quad_weights.reshape(1, LATS), vert_rates.reshape(1, LEV), vert_proj, vert_recon, fourier, legendre)
+    )(*[pltpu.with_memory_space_constraint(v, pltpu.HBM) for v in (
+        slot_wave.reshape(total // 128, 128), quad_weights.reshape(1, LATS), vert_rates.reshape(1, LEV),
+        vert_proj, vert_recon, jnp.transpose(fourier, (1, 2, 0)), legendre)])
     returned, spectral = pl.pallas_call(
         place_kernel,
         out_shape=(jax.ShapeDtypeStruct(fourier.shape, BF16), jax.ShapeDtypeStruct(spectral.shape, BF16)),

time: 85.8 us -> 83.1 us (0.969)
  local copies, waits for them, and re-layouts: 3.72 us -> 1.66 us
    unnamed x12 -> x3, local copies, waits for them, and re-layouts: 3.72 us -> 1.66 us
where the time goes in v3:
time: 83.1 us; the launch traced here: 82.9 us
  Pallas kernels  80.6 us (97%)
  local copies, waits for them, and re-layouts  1.66 us (2%)
    pallas_call x1, Pallas kernels, per_device(): pl.pallas_call(exchange_kernel, out_shape=(jax.ShapeDtypeStruct((2 * LEV,...  77.5 us
    pallas_call x1, Pallas kernels, per_device(): pl.pallas_call(place_kernel, out_shape=(jax.ShapeDtypeStruct(fourier.shap...  3.11 us
    unnamed x3, local copies, waits for them, and re-layouts  1.66 us

profile of v3, /device:TPU:1, one launch (start us, length us, event | category | flops | bytes accessed | tf_op | source)
XLA Modules:
  0.0 82.9 jit_solution(11320457664398077391)
XLA Ops:
  0.6 0.0 copy-start
  0.6 77.5 %exchange.1 = (bf16[192,768]{1,0:T(8,128)(2,1)S(1)}, bf16[16,12,8,128]{3,2,1,0:T(8,128)(2,1)S(1)}, bf16[24,7,8,128]{3,2,1,0:T(8,128)(2,1)S(1)}) custom-call(s32[6,128]{1,0:T(8,128)} %bitcast.5, f32[1,56]{1,0:T(1,128)} %bitcast.7, f32[1,96]{1,0:T(1,128)} %bitcast.8, f32[96,96]{1,0:T(8,128)} %proj_hbm.1, f32[96,96]{1,0:T(8,128)} %recon_hbm.1, ...), custom_call_target="tpu_custom_call" | custom-call | tf_op jit(solution)/shard_map/exchange/pallas_call | solution.py:368
  78.1 0.0 copy-done
  78.1 3.1 %place.1 = (bf16[768,8,56]{2,1,0:T(8,128)(2,1)S(1)}, bf16[192,768]{1,0:T(8,128)(2,1)}) custom-call(s32[768]{0:T(1024)S(1)} %copy-done, bf16[16,12,8,128]{3,2,1,0:T(8,128)(2,1)S(1)} %get-tuple-element.7.from_a, bf16[24,7,8,128]{3,2,1,0:T(8,128)(2,1)S(1)} %get-tuple-element.8.from_b, bf16[192,768]{1,0:T(8,128)(2,1)S(1)} %get-tuple-element.9.solved), custom_call_target="tpu_custom_call" | custom-call | tf_op jit(solution)/shard_map/place/pallas_call | solution.py:401
  81.2 1.7 %copy.9 = bf16[768,8,56]{0,2,1:T(8,128)(2,1)} copy(bf16[768,8,56]{2,1,0:T(8,128)(2,1)S(1)} %get-tuple-element.13) | data formatting | bytes 1376256
Async XLA Ops:
  0.6 77.5 %copy-start = (s32[768]{0:T(1024)S(1)}, s32[768]{0:T(1024)}, u32[]{:S(2)}) copy-start(s32[768]{0:T(1024)} %waves.1) | copy-start | bytes 9220

commit v4 on v3

--- a/solution.py
+++ b/solution.py
@@ -18,7 +18,9 @@
 TAIL = 128 - PAIR
 ND = HB // 2 - 1
 SKEW = 8 * (ND + 1) + 8
-Z_ORDER = (6, 5, -5, 4, -4, 3, -3, 2, -2, 1, -1, 0)
+FAR = 4
+CHUNKS = ((0, 5), (5, 7))
+Z_ORDERS = ((6, 5, -5, 4, -4), (3, -3, 2, -2, 1, -1, 0))
 Y_ORDER = (4, 3, -3, 2, -2, 1, -1, 0)
 
 
@@ -34,12 +36,16 @@
     return pltpu.roll(v, by % 128, 1)
 
 
-def dense_to_pair(src, dst, z):
+def chip_of(z, t):
+    return lax.rem(z + FAR + t, NZ)
+
+
+def dense_to_pair(src, dst, z, t):
     lane = lanes()
     low = lane < LATS
     halves = []
     for core in range(2):
-        f = 2 * z + core
+        f = 2 * chip_of(z, t) + core
         tiles = [src[f, i].astype(F32) for i in range(ND)]
         last = roll(tiles[0], TAIL)
         for i in range(1, ND):
@@ -47,16 +53,16 @@
         halves.append(tiles + [last])
     for i in range(ND + 1):
         one, two = halves[0][i], halves[1][i]
-        dst[2 * i, z] = jnp.where(low, one, roll(two, LATS)).astype(BF16)
-        dst[2 * i + 1, z] = jnp.where(low, roll(one, -LATS), two).astype(BF16)
-
-
-def pair_to_dense(src, z):
+        dst[2 * i, t] = jnp.where(low, one, roll(two, LATS)).astype(BF16)
+        dst[2 * i + 1, t] = jnp.where(low, roll(one, -LATS), two).astype(BF16)
+
+
+def pair_to_dense(src, t):
     lane = lanes()
     low, body = lane < LATS, lane < PAIR
     first, second = [], []
     for i in range(ND + 1):
-        even, odd = src[2 * i, z].astype(F32), src[2 * i + 1, z].astype(F32)
+        even, odd = src[2 * i, t].astype(F32), src[2 * i + 1, t].astype(F32)
         first.append(jnp.where(low, even, roll(odd, LATS)))
         second.append(jnp.where(low, roll(even, -LATS), odd))
     out = []
@@ -77,9 +83,10 @@
 
 
 def near_exact(left, right):
+    n = left.shape[0] // 2
     high, low = parts_of(right)
-    small = jnp.dot(left[0], low, preferred_element_type=F32) + jnp.dot(left[1], high, preferred_element_type=F32)
-    return jnp.dot(left[0], high, preferred_element_type=F32) + small
+    both = jnp.dot(left, high, preferred_element_type=F32)
+    return both[:n] + (both[n:] + jnp.dot(left[:n], low, preferred_element_type=F32))
 
 
 def exchange_kernel(
@@ -106,10 +113,15 @@
         copy.start()
     fetch.start()
 
-    for i in range(1, NF):
-        pl.semaphore_signal(barrier, 1, device_id=(b, lax.rem(f + i, NF)), device_id_type=MESH)
-    for i in range(1, NB):
-        pl.semaphore_signal(barrier, 1, device_id=(lax.rem(b + i, NB), f), device_id_type=MESH)
+    greeted = [(abs(d), "field", d, k) for order in Z_ORDERS for d in order for k in range(2) if (d, k) != (0, 0)]
+    greeted += [
+        (min(dx, NX - dx) + abs(dy), "band", dx, dy) for dy in Y_ORDER for dx in range(NX) if (dx, dy) != (0, 0)]
+    for _, axis, one, two in sorted(greeted, key=lambda item: -item[0]):
+        if axis == "field":
+            to = (b, lax.rem(z + one + NZ, NZ) * 2 + lax.rem(core + two, 2))
+        else:
+            to = (lax.rem(x + one, NX) * NY + lax.rem(y + two + NY, NY), f)
+        pl.semaphore_signal(barrier, 1, device_id=to, device_id_type=MESH)
 
     table = []
     for part in range(2):
@@ -173,7 +185,7 @@
 
     def pack_pair(j, carry):
         for k in range(NZ):
-            sb1[j, k] = tiles_b[pl.ds(pl.multiple_of((j * NZ + k) * 8, 8), 8), :].astype(BF16)
+            sb1[j, k] = tiles_b[pl.ds(pl.multiple_of((j * NZ + chip_of(z, k)) * 8, 8), 8), :].astype(BF16)
         return carry
 
     def pack_dense(field, carry):
@@ -191,26 +203,29 @@
             src_ref=src, dst_ref=dst, send_sem=send_sem.at[phase], recv_sem=recv_sem.at[phase],
             device_id=device, device_id_type=MESH).start()
 
-    def send_field(src, dst, phase):
-        for d in Z_ORDER:
+    def send_field(src, dst, phase, chunk):
+        for d in Z_ORDERS[chunk]:
             for k in range(2):
                 if d == 0 and k == 0:
                     continue
                 to = lax.rem(z + d + NZ, NZ) * 2 + lax.rem(core + k, 2)
-                send(src.at[to], dst.at[f], phase, (b, to))
-
-    def send_band(src, dst, phase, same):
-        steps = (2, 0) if same else (1, 3)
+                send(src.at[to], dst.at[f], 2 * phase + chunk, (b, to))
+        if chunk == 1:
+            dst[f] = src[f]
+
+    def send_band(src, dst, phase, chunk, same):
+        part = pl.ds(*CHUNKS[chunk])
         for dy in Y_ORDER:
-            for dx in steps:
+            for dx in (2, 0) if same else (1, 3):
                 if dx == 0 and dy == 0:
                     continue
                 to_x, to_y = lax.rem(x + dx, NX), lax.rem(y + dy + NY, NY)
                 to = (to_x // 2) * NY + to_y
-                send(src.at[to], dst.at[mine], phase, (to_x * NY + to_y, f))
-
-    def wait_all(ref, phase, count, received):
-        some = ref.at[pl.ds(0, count)]
+                send(src.at[to, part], dst.at[mine, part], 2 * phase + chunk, (to_x * NY + to_y, f))
+        if same:
+            dst[mine, part] = src[mine, part]
+
+    def wait_some(some, phase, received):
         copy = pltpu.make_async_remote_copy(
             src_ref=some, dst_ref=some, send_sem=send_sem.at[phase], recv_sem=recv_sem.at[phase],
             device_id=(b, f), device_id_type=MESH)
@@ -219,66 +234,82 @@
         else:
             copy.wait_send()
 
-    def over_z(body):
+    def wait_field(ref, phase, chunk, received=True):
+        wait_some(ref.at[pl.ds(0, (10, 13)[chunk])], 2 * phase + chunk, received)
+
+    def wait_band(ref, phase, chunk, same, received=True):
+        wait_some(ref.at[pl.ds(0, HB - 1 if same else HB), pl.ds(*CHUNKS[chunk])], 2 * phase + chunk, received)
+
+    def over_chunk(chunk, body):
+        first, count = CHUNKS[chunk]
+
         def step(k, carry):
-            body(k)
+            body(first + k)
             return carry
 
-        lax.fori_loop(0, NZ, step, 0, unroll=3)
-
-    def put_dense(src, dst):
-        def body(k):
-            out = pair_to_dense(src, k)
+        lax.fori_loop(0, count, step, 0, unroll=count)
+
+    def put_dense(src, dst, chunk):
+        def body(t):
+            out = pair_to_dense(src, t)
             for c in range(2):
                 for i in range(ND):
-                    dst[2 * k + c, i] = out[c][i].astype(BF16)
-
-        over_z(body)
-
-    send_field(sa1, ra1, 0)
+                    dst[2 * chip_of(z, t) + c, i] = out[c][i].astype(BF16)
+
+        over_chunk(chunk, body)
+
+    def put_pair(src, dst, chunk):
+        over_chunk(chunk, functools.partial(dense_to_pair, src, dst, z))
+
+    for chunk in range(2):
+        send_field(sa1, ra1, 0, chunk)
     lax.fori_loop(0, NY * NZ // 8, rows_pair, 0, unroll=2)
     lax.fori_loop(0, HB, pack_pair, 0, unroll=2)
-    send_band(sb1, rb1, 1, False)
-    ra1[f] = sa1[f]
-
-    wait_all(rb1, 1, HB, True)
-    put_dense(rb1, sb2)
-    send_field(sb2, rb2, 2)
-    rb2[f] = sb2[f]
-
-    wait_all(ra1, 0, NF - 1, True)
-    over_z(functools.partial(dense_to_pair, ra1, sa2))
-    send_band(sa2, ra2, 3, True)
-    ra2[mine] = sa2[mine]
-
+    for chunk in range(2):
+        send_band(sb1, rb1, 1, chunk, False)
+
+    def second_phase(in_b, out_b, end_b, in_a, out_a, end_a, phase):
+        for chunk in range(2):
+            wait_band(in_b, phase + 1, chunk, False)
+            put_dense(in_b, out_b, chunk)
+            send_field(out_b, end_b, phase + 2, chunk)
+            wait_field(in_a, phase, chunk)
+            put_pair(in_a, out_a, chunk)
+            send_band(out_a, end_a, phase + 3, chunk, True)
+
+    second_phase(rb1, sb2, rb2, ra1, sa2, ra2, 0)
     for copy in table:
         copy.wait()
     step_n = 256
     half_k = ND * 128
 
-    wait_all(ra2, 3, HB - 1, True)
-
-    def left_a(k):
-        out = pair_to_dense(ra2, k)
+    def left_a(t):
+        out = pair_to_dense(ra2, t)
+        row = pl.multiple_of(16 * chip_of(z, t), 16)
         for i in range(ND):
             both = jnp.concatenate([out[0][i], out[1][i]], axis=0)
-            left[pl.ds(pl.multiple_of(16 * k, 16), 16), 128 * i:128 * (i + 1)] = both.astype(BF16)
-
-    over_z(left_a)
+            left[pl.ds(row, 16), 128 * i:128 * (i + 1)] = both.astype(BF16)
+
+    for chunk in range(2):
+        wait_band(ra2, 3, chunk, True)
+        over_chunk(chunk, left_a)
     for n in range(0, total, step_n):
         direct[:, n:n + step_n] = jnp.dot(
             left[:, :half_k], legendre[:half_k, n:n + step_n], preferred_element_type=F32)
 
-    wait_all(rb2, 2, NF - 1, True)
-
-    def left_b(k):
+    for chunk in range(2):
+        wait_field(rb2, 2, chunk)
+
+    def left_b(k, carry):
         for i in range(ND):
             both = jnp.concatenate([rb2[2 * k, i].astype(F32), rb2[2 * k + 1, i].astype(F32)], axis=0)
             left[pl.ds(pl.multiple_of(16 * k, 16), 16), half_k + 128 * i:half_k + 128 * (i + 1)] = both.astype(BF16)
-
-    over_z(left_b)
+        return carry
+
+    lax.fori_loop(0, NZ, left_b, 0, unroll=3)
     rate = turned(rates[...])
-    proj_parts, recon_parts = parts_of(proj[...]), parts_of(recon[...])
+    proj_parts = jnp.concatenate(parts_of(proj[...]), axis=0)
+    recon_parts = jnp.concatenate(parts_of(recon[...]), axis=0)
     place_of = lax.broadcasted_iota(jnp.int32, waves.shape, 0) * 128 + lax.broadcasted_iota(jnp.int32, waves.shape, 1)
     mine_only = jnp.where(place_of == b * NF + f, waves[...].astype(F32), 0.0)
     my_wave = jnp.sum(jnp.sum(mine_only, axis=1, keepdims=True), axis=0, keepdims=True)
@@ -300,36 +331,31 @@
                 spectral[...], legendre[row:row + 128, :], (((1,), (1,)), ((), ())), preferred_element_type=F32)
             out[:, i] = made.reshape(NF, 8, 128).astype(BF16)
 
+    back(0, xa)
+    for chunk in range(2):
+        send_field(xa, ya, 4, chunk)
     back(1, xb)
-    over_z(functools.partial(dense_to_pair, xb, yb))
-    send_band(yb, zb, 5, False)
-    back(0, xa)
-    send_field(xa, ya, 4)
-    ya[f] = xa[f]
-
-    wait_all(zb, 5, HB, True)
-    put_dense(zb, vb)
-    send_field(vb, last_b, 6)
-    last_b[f] = vb[f]
-
-    wait_all(ya, 4, NF - 1, True)
-    over_z(functools.partial(dense_to_pair, ya, za))
-    send_band(za, last_a, 7, True)
-    last_a[mine] = za[mine]
-
-    wait_all(last_a, 7, HB - 1, True)
-    wait_all(last_b, 6, NF - 1, True)
-    for ref, phase, count in (
-        (sa1, 0, NF - 1), (sb1, 1, HB), (sb2, 2, NF - 1), (sa2, 3, HB - 1),
-        (xa, 4, NF - 1), (yb, 5, HB), (vb, 6, NF - 1), (za, 7, HB - 1),
-    ):
-        wait_all(ref, phase, count, False)
+    for chunk in range(2):
+        put_pair(xb, yb, chunk)
+        send_band(yb, zb, 5, chunk, False)
+
+    second_phase(zb, vb, last_b, ya, za, last_a, 4)
+    for chunk in range(2):
+        wait_band(last_a, 7, chunk, True)
+    for chunk in range(2):
+        wait_field(last_b, 6, chunk)
+    for chunk in range(2):
+        for ref, phase in ((sa1, 0), (sb2, 2), (xa, 4), (vb, 6)):
+            wait_field(ref, phase, chunk, received=False)
+        for ref, phase, same in ((sb1, 1, False), (sa2, 3, True), (yb, 5, False), (za, 7, True)):
+            wait_band(ref, phase, chunk, same, received=False)
 
 
 def place_kernel(waves, from_a, from_b, solved, returned, spectral):
     spectral[...] = solved[...]
     b = lax.axis_index("band")
     parity = lax.rem(b // NY, 2)
+    z = lax.axis_index("field") // 2
     lane = lanes()
 
     def put(band, field, tile):
@@ -339,8 +365,8 @@
         band = (parity + 2 * (j // NY)) * NY + lax.rem(j, NY)
         for k in range(NZ):
             tile = from_a[j, k].astype(F32)
-            put(band, 2 * k, tile)
-            put(band, 2 * k + 1, roll(tile, -LATS))
+            put(band, 2 * chip_of(z, k), tile)
+            put(band, 2 * chip_of(z, k) + 1, roll(tile, -LATS))
         return carry
 
     lax.fori_loop(0, HB, one_a, 0, unroll=4)
@@ -391,7 +417,7 @@
             pltpu.VMEM((HB * NZ * 8, 128), F32),
         ]
         + [pltpu.VMEM(shape, BF16) for shape in buffers]
-        + [pltpu.SemaphoreType.DMA((5,)), pltpu.SemaphoreType.DMA, pltpu.SemaphoreType.DMA, pltpu.SemaphoreType.DMA((8,)), pltpu.SemaphoreType.DMA((8,))],
+        + [pltpu.SemaphoreType.DMA((5,)), pltpu.SemaphoreType.DMA, pltpu.SemaphoreType.DMA, pltpu.SemaphoreType.DMA((16,)), pltpu.SemaphoreType.DMA((16,))],
         compiler_params=pltpu.CompilerParams(
             collective_id=0, has_side_effects=True, vmem_limit_bytes=55_000_000),
         name="exchange",

time: 83.1 us -> 78.1 us (0.940)
  Pallas kernels: 80.6 us -> 75.6 us
    pallas_call x1, Pallas kernels: 77.5 us -> 72.3 us  [per_device(): pl.pallas_call(exchange_kernel, out_shape=(jax.ShapeDtypeStruct((2 * LEV,...]
where the time goes in v4:
time: 78.1 us; the launch traced here: 78 us
  Pallas kernels  75.6 us (97%)
  local copies, waits for them, and re-layouts  1.66 us (2%)
    pallas_call x1, Pallas kernels, per_device(): pl.pallas_call(exchange_kernel, out_shape=(jax.ShapeDtypeStruct((2 * LEV,...  72.3 us
    pallas_call x1, Pallas kernels, per_device(): pl.pallas_call(place_kernel, out_shape=(jax.ShapeDtypeStruct(fourier.shap...  3.34 us
    unnamed x3, local copies, waits for them, and re-layouts  1.66 us

profile of v4, /device:TPU:1, one launch (start us, length us, event | category | flops | bytes accessed | tf_op | source)
XLA Modules:
  0.0 78.0 jit_solution(3803030951511062681)
XLA Ops:
  0.6 0.0 copy-start
  0.6 72.3 %exchange.1 = (bf16[192,768]{1,0:T(8,128)(2,1)S(1)}, bf16[16,12,8,128]{3,2,1,0:T(8,128)(2,1)S(1)}, bf16[24,7,8,128]{3,2,1,0:T(8,128)(2,1)S(1)}) custom-call(s32[6,128]{1,0:T(8,128)} %bitcast.5, f32[1,56]{1,0:T(1,128)} %bitcast.7, f32[1,96]{1,0:T(1,128)} %bitcast.8, f32[96,96]{1,0:T(8,128)} %proj_hbm.1, f32[96,96]{1,0:T(8,128)} %recon_hbm.1, ...), custom_call_target="tpu_custom_call" | custom-call | tf_op jit(solution)/shard_map/exchange/pallas_call | solution.py:394
  72.9 0.0 copy-done
  73.0 3.3 %place.1 = (bf16[768,8,56]{2,1,0:T(8,128)(2,1)S(1)}, bf16[192,768]{1,0:T(8,128)(2,1)}) custom-call(s32[768]{0:T(1024)S(1)} %copy-done, bf16[16,12,8,128]{3,2,1,0:T(8,128)(2,1)S(1)} %get-tuple-element.7.from_a, bf16[24,7,8,128]{3,2,1,0:T(8,128)(2,1)S(1)} %get-tuple-element.8.from_b, bf16[192,768]{1,0:T(8,128)(2,1)S(1)} %get-tuple-element.9.solved), custom_call_target="tpu_custom_call" | custom-call | tf_op jit(solution)/shard_map/place/pallas_call | solution.py:427
  76.3 1.7 %copy.9 = bf16[768,8,56]{0,2,1:T(8,128)(2,1)} copy(bf16[768,8,56]{2,1,0:T(8,128)(2,1)S(1)} %get-tuple-element.13) | data formatting | bytes 1376256
Async XLA Ops:
  0.6 72.3 %copy-start = (s32[768]{0:T(1024)S(1)}, s32[768]{0:T(1024)}, u32[]{:S(2)}) copy-start(s32[768]{0:T(1024)} %waves.1) | copy-start | bytes 9220

commit v5 on v4

--- a/solution.py
+++ b/solution.py
@@ -92,7 +92,8 @@
 def exchange_kernel(
     waves_hbm, quad_hbm, rates_hbm, proj_hbm, recon_hbm, fourier_hbm, legendre_hbm,
     spectral, last_a, last_b,
-    waves, quad, rates, proj, recon, legendre, left, direct, fourier, weighted, chosen, gathered, tiles_a, tiles_b,
+    waves, quad, rates, proj, recon, gamma, keep, proj_parts, recon_parts, modes,
+    legendre, left, direct, fourier, weighted, chosen, gathered, tiles_a, tiles_b,
     sa1, ra1, sa2, ra2, sb1, rb1, sb2, rb2,
     xa, ya, za, xb, yb, zb, vb,
     small_sem, local_sem, fetch_sem, send_sem, recv_sem,
@@ -196,6 +197,8 @@
 
     lax.fori_loop(0, ND + 1, rows_dense, 0, unroll=2)
     lax.fori_loop(0, NF, pack_dense, 0, unroll=3)
+    lax.fori_loop(0, NY * NZ // 8, rows_pair, 0, unroll=2)
+    lax.fori_loop(0, HB, pack_pair, 0, unroll=2)
     pl.semaphore_wait(barrier, NB + NF - 2)
 
     def send(src, dst, phase, device):
@@ -263,10 +266,16 @@
 
     for chunk in range(2):
         send_field(sa1, ra1, 0, chunk)
-    lax.fori_loop(0, NY * NZ // 8, rows_pair, 0, unroll=2)
-    lax.fori_loop(0, HB, pack_pair, 0, unroll=2)
     for chunk in range(2):
         send_band(sb1, rb1, 1, chunk, False)
+    order = lax.broadcasted_iota(jnp.int32, (LEV, total), 1).astype(F32)
+    gamma[...] = 1.0 / (1.0 + turned(rates[...]) * (order * (order + 1.0) / float(total * total)))
+    place_of = lax.broadcasted_iota(jnp.int32, waves.shape, 0) * 128 + lax.broadcasted_iota(jnp.int32, waves.shape, 1)
+    mine_only = jnp.where(place_of == b * NF + f, waves[...].astype(F32), 0.0)
+    my_wave = jnp.sum(jnp.sum(mine_only, axis=1, keepdims=True), axis=0, keepdims=True)
+    keep[...] = jnp.where(order[:1] >= my_wave, 1.0, 0.0)
+    proj_parts[...] = jnp.concatenate(parts_of(proj[...]), axis=0)
+    recon_parts[...] = jnp.concatenate(parts_of(recon[...]), axis=0)
 
     def second_phase(in_b, out_b, end_b, in_a, out_a, end_a, phase):
         for chunk in range(2):
@@ -307,29 +316,25 @@
         return carry
 
     lax.fori_loop(0, NZ, left_b, 0, unroll=3)
-    rate = turned(rates[...])
-    proj_parts = jnp.concatenate(parts_of(proj[...]), axis=0)
-    recon_parts = jnp.concatenate(parts_of(recon[...]), axis=0)
-    place_of = lax.broadcasted_iota(jnp.int32, waves.shape, 0) * 128 + lax.broadcasted_iota(jnp.int32, waves.shape, 1)
-    mine_only = jnp.where(place_of == b * NF + f, waves[...].astype(F32), 0.0)
-    my_wave = jnp.sum(jnp.sum(mine_only, axis=1, keepdims=True), axis=0, keepdims=True)
     for n in range(0, total, step_n):
-        part = direct[:, n:n + step_n] + jnp.dot(
+        direct[:, n:n + step_n] += jnp.dot(
             left[:, half_k:], legendre[half_k:, n:n + step_n], preferred_element_type=F32)
-        order = (lax.broadcasted_iota(jnp.int32, (LEV, step_n), 1) + n).astype(F32)
-        gamma = 1.0 / (1.0 + rate * (order * (order + 1.0) / float(total * total)))
-        for c in range(2):
-            modes = gamma * near_exact(proj_parts, part[LEV * c:LEV * (c + 1)])
-            solved = near_exact(recon_parts, modes)
-            kept = jnp.where(order >= my_wave, solved, 0.0)
-            spectral[LEV * c:LEV * (c + 1), n:n + step_n] = kept.astype(BF16)
+    pieces = [(LEV * c, n) for n in range(0, total, step_n) for c in range(2)]
+    for row, n in pieces:
+        found = near_exact(proj_parts[...], direct[row:row + LEV, n:n + step_n])
+        modes[row:row + LEV, n:n + step_n] = gamma[:, n:n + step_n] * found
+    for row, n in pieces:
+        solved = near_exact(recon_parts[...], modes[row:row + LEV, n:n + step_n])
+        spectral[row:row + LEV, n:n + step_n] = jnp.where(keep[:, n:n + step_n] > 0.5, solved, 0.0).astype(BF16)
 
     def back(part, out):
-        for i in range(ND):
+        for i in range(0, ND, 2):
+            count = min(2, ND - i)
             row = (part * ND + i) * 128
             made = lax.dot_general(
-                spectral[...], legendre[row:row + 128, :], (((1,), (1,)), ((), ())), preferred_element_type=F32)
-            out[:, i] = made.reshape(NF, 8, 128).astype(BF16)
+                spectral[...], legendre[row:row + 128 * count, :], (((1,), (1,)), ((), ())), preferred_element_type=F32)
+            for k in range(count):
+                out[:, i + k] = made[:, 128 * k:128 * (k + 1)].reshape(NF, 8, 128).astype(BF16)
 
     back(0, xa)
     for chunk in range(2):
@@ -351,7 +356,7 @@
             wait_band(ref, phase, chunk, same, received=False)
 
 
-def place_kernel(waves, from_a, from_b, solved, returned, spectral):
+def place_kernel(waves, from_a, from_b, solved, returned, spectral, placed):
     spectral[...] = solved[...]
     b = lax.axis_index("band")
     parity = lax.rem(b // NY, 2)
@@ -359,7 +364,7 @@
     lane = lanes()
 
     def put(band, field, tile):
-        returned[waves[band * NF + field]] = tile[:, :LATS].astype(BF16)
+        placed[pl.ds(pl.multiple_of(waves[band * NF + field] * 8, 8), 8), :] = tile
 
     def one_a(j, carry):
         band = (parity + 2 * (j // NY)) * NY + lax.rem(j, NY)
@@ -382,6 +387,14 @@
         return carry
 
     lax.fori_loop(0, NF, one_b, 0, unroll=4)
+
+    total = returned.shape[2]
+    rows = lax.broadcasted_iota(jnp.int32, (LATS, 128), 0)
+    same = jnp.where(rows == lax.broadcasted_iota(jnp.int32, (LATS, 128), 1), 1.0, 0.0).astype(BF16)
+    for r in range(8):
+        waves_by_lat = placed[pl.ds(r, total, stride=8), :].astype(BF16)
+        returned[r] = lax.dot_general(
+            same, waves_by_lat, (((1,), (1,)), ((), ())), preferred_element_type=F32).astype(BF16)
 
 
 def per_device(fourier, quad_weights, legendre, slot_wave, vert_proj, vert_recon, vert_rates):
@@ -406,6 +419,11 @@
             pltpu.VMEM((1, LEV), F32),
             pltpu.VMEM((LEV, LEV), F32),
             pltpu.VMEM((LEV, LEV), F32),
+            pltpu.VMEM((LEV, total), F32),
+            pltpu.VMEM((1, total), F32),
+            pltpu.VMEM((2 * LEV, LEV), BF16),
+            pltpu.VMEM((2 * LEV, LEV), BF16),
+            pltpu.VMEM((2 * LEV, total), F32),
             pltpu.VMEM((nlat, total), BF16),
             pltpu.VMEM((2 * LEV, nlat), BF16),
             pltpu.VMEM((2 * LEV, total), F32),
@@ -426,13 +444,14 @@
         vert_proj, vert_recon, jnp.transpose(fourier, (1, 2, 0)), legendre)])
     returned, spectral = pl.pallas_call(
         place_kernel,
-        out_shape=(jax.ShapeDtypeStruct(fourier.shape, BF16), jax.ShapeDtypeStruct(spectral.shape, BF16)),
+        out_shape=(jax.ShapeDtypeStruct((8, LATS, total), BF16), jax.ShapeDtypeStruct(spectral.shape, BF16)),
         in_specs=[smem, vmem, vmem, vmem],
         out_specs=[vmem, vmem],
+        scratch_shapes=[pltpu.VMEM((total * 8, 128), F32)],
         compiler_params=pltpu.CompilerParams(vmem_limit_bytes=16 * 1024 * 1024),
         name="place",
     )(slot_wave, last_a, last_b, spectral)
-    return spectral.reshape(1, 2, LEV, total), returned
+    return spectral.reshape(1, 2, LEV, total), jnp.transpose(returned, (2, 0, 1))
 
 
 def solution(mesh):

time: 78.1 us -> 76 us (0.973)
  local copies, waits for them, and re-layouts: 1.66 us -> 0.01 us
    unnamed x3 -> x2, local copies, waits for them, and re-layouts: 1.66 us -> 0.01 us
    pallas_call x1, Pallas kernels: 72.3 us -> 70.8 us  [per_device(): pl.pallas_call(exchange_kernel, out_shape=(jax.ShapeDtypeStruct((2 * LEV,...]
    pallas_call x1, Pallas kernels: 3.34 us -> 4.33 us  [per_device(): pl.pallas_call(place_kernel, out_shape=(jax.ShapeDtypeStruct((8, LATS, to...]
where the time goes in v5:
time: 76 us; the launch traced here: 75.8 us
  Pallas kernels  75.1 us (99%)
    pallas_call x1, Pallas kernels, per_device(): pl.pallas_call(exchange_kernel, out_shape=(jax.ShapeDtypeStruct((2 * LEV,...  70.8 us
    pallas_call x1, Pallas kernels, per_device(): pl.pallas_call(place_kernel, out_shape=(jax.ShapeDtypeStruct((8, LATS, to...  4.33 us

profile of v5, /device:TPU:1, one launch (start us, length us, event | category | flops | bytes accessed | tf_op | source)
XLA Modules:
  0.0 75.8 jit_solution(15052499920796056399)
XLA Ops:
  0.6 0.0 copy-start
  0.6 70.8 %exchange.1 = (bf16[192,768]{1,0:T(8,128)(2,1)S(1)}, bf16[16,12,8,128]{3,2,1,0:T(8,128)(2,1)S(1)}, bf16[24,7,8,128]{3,2,1,0:T(8,128)(2,1)S(1)}) custom-call(s32[6,128]{1,0:T(8,128)} %bitcast.6, f32[1,56]{1,0:T(1,128)} %bitcast.8, f32[1,96]{1,0:T(1,128)} %bitcast.9, f32[96,96]{1,0:T(8,128)} %proj_hbm.1, f32[96,96]{1,0:T(8,128)} %recon_hbm.1, ...), custom_call_target="tpu_custom_call" | custom-call | tf_op jit(solution)/shard_map/exchange/pallas_call | solution.py:407
  71.5 0.0 copy-done
  71.5 4.3 %place.1 = (bf16[8,56,768]{2,1,0:T(8,128)(2,1)}, bf16[192,768]{1,0:T(8,128)(2,1)}) custom-call(s32[768]{0:T(1024)S(1)} %copy-done, bf16[16,12,8,128]{3,2,1,0:T(8,128)(2,1)S(1)} %get-tuple-element.7.from_a, bf16[24,7,8,128]{3,2,1,0:T(8,128)(2,1)S(1)} %get-tuple-element.8.from_b, bf16[192,768]{1,0:T(8,128)(2,1)S(1)} %get-tuple-element.9.solved), custom_call_target="tpu_custom_call" | custom-call | tf_op jit(solution)/shard_map/place/pallas_call | solution.py:445
Async XLA Ops:
  0.6 70.8 %copy-start = (s32[768]{0:T(1024)S(1)}, s32[768]{0:T(1024)}, u32[]{:S(2)}) copy-start(s32[768]{0:T(1024)} %waves.1) | copy-start | bytes 9220

commit v6 on v5

--- a/solution.py
+++ b/solution.py
@@ -356,8 +356,9 @@
             wait_band(ref, phase, chunk, same, received=False)
 
 
-def place_kernel(waves, from_a, from_b, solved, returned, spectral, placed):
-    spectral[...] = solved[...]
+def place_kernel(waves, from_a, from_b, solved, returned, spectral, placed, made, out_sem):
+    copies = [pltpu.make_async_copy(solved, spectral, out_sem.at[8])]
+    copies[0].start()
     b = lax.axis_index("band")
     parity = lax.rem(b // NY, 2)
     z = lax.axis_index("field") // 2
@@ -366,15 +367,17 @@
     def put(band, field, tile):
         placed[pl.ds(pl.multiple_of(waves[band * NF + field] * 8, 8), 8), :] = tile
 
+    fields = [2 * chip_of(z, k) for k in range(NZ)]
+
     def one_a(j, carry):
         band = (parity + 2 * (j // NY)) * NY + lax.rem(j, NY)
         for k in range(NZ):
             tile = from_a[j, k].astype(F32)
-            put(band, 2 * chip_of(z, k), tile)
-            put(band, 2 * chip_of(z, k) + 1, roll(tile, -LATS))
-        return carry
-
-    lax.fori_loop(0, HB, one_a, 0, unroll=4)
+            put(band, fields[k], tile)
+            put(band, fields[k] + 1, roll(tile, -LATS))
+        return carry
+
+    lax.fori_loop(0, HB, one_a, 0, unroll=8)
 
     def one_b(field, carry):
         tiles = [from_b[field, i].astype(F32) for i in range(ND)]
@@ -386,15 +389,19 @@
             put(band_of(1 - parity, 2 * i + 1), field, roll(tile, -LATS))
         return carry
 
-    lax.fori_loop(0, NF, one_b, 0, unroll=4)
+    lax.fori_loop(0, NF, one_b, 0, unroll=8)
 
     total = returned.shape[2]
     rows = lax.broadcasted_iota(jnp.int32, (LATS, 128), 0)
     same = jnp.where(rows == lax.broadcasted_iota(jnp.int32, (LATS, 128), 1), 1.0, 0.0).astype(BF16)
     for r in range(8):
         waves_by_lat = placed[pl.ds(r, total, stride=8), :].astype(BF16)
-        returned[r] = lax.dot_general(
+        made[r] = lax.dot_general(
             same, waves_by_lat, (((1,), (1,)), ((), ())), preferred_element_type=F32).astype(BF16)
+        copies.append(pltpu.make_async_copy(made.at[r], returned.at[r], out_sem.at[r]))
+        copies[-1].start()
+    for copy in copies:
+        copy.wait()
 
 
 def per_device(fourier, quad_weights, legendre, slot_wave, vert_proj, vert_recon, vert_rates):
@@ -446,8 +453,9 @@
         place_kernel,
         out_shape=(jax.ShapeDtypeStruct((8, LATS, total), BF16), jax.ShapeDtypeStruct(spectral.shape, BF16)),
         in_specs=[smem, vmem, vmem, vmem],
-        out_specs=[vmem, vmem],
-        scratch_shapes=[pltpu.VMEM((total * 8, 128), F32)],
+        out_specs=[hbm, hbm],
+        scratch_shapes=[
+            pltpu.VMEM((total * 8, 128), F32), pltpu.VMEM((8, LATS, total), BF16), pltpu.SemaphoreType.DMA((9,))],
         compiler_params=pltpu.CompilerParams(vmem_limit_bytes=16 * 1024 * 1024),
         name="place",
     )(slot_wave, last_a, last_b, spectral)

time: 76 us -> 75.4 us (level)
  no operation moved by 1% of the time
where the time goes in v6:
time: 75.4 us; the launch traced here: 75.3 us
  Pallas kernels  74.6 us (99%)
    pallas_call x1, Pallas kernels, per_device(): pl.pallas_call(exchange_kernel, out_shape=(jax.ShapeDtypeStruct((2 * LEV,...  70.8 us
    pallas_call x1, Pallas kernels, per_device(): pl.pallas_call(place_kernel, out_shape=(jax.ShapeDtypeStruct((8, LATS, to...  3.81 us

profile of v6, /device:TPU:1, one launch (start us, length us, event | category | flops | bytes accessed | tf_op | source)
XLA Modules:
  0.0 75.3 jit_solution(16247416077291951579)
XLA Ops:
  0.6 0.0 copy-start
  0.6 70.8 %exchange.1 = (bf16[192,768]{1,0:T(8,128)(2,1)S(1)}, bf16[16,12,8,128]{3,2,1,0:T(8,128)(2,1)S(1)}, bf16[24,7,8,128]{3,2,1,0:T(8,128)(2,1)S(1)}) custom-call(s32[6,128]{1,0:T(8,128)} %bitcast.6, f32[1,56]{1,0:T(1,128)} %bitcast.8, f32[1,96]{1,0:T(1,128)} %bitcast.9, f32[96,96]{1,0:T(8,128)} %proj_hbm.1, f32[96,96]{1,0:T(8,128)} %recon_hbm.1, ...), custom_call_target="tpu_custom_call" | custom-call | tf_op jit(solution)/shard_map/exchange/pallas_call | solution.py:414
  71.5 0.0 copy-done
  71.5 3.8 %place.1 = (bf16[8,56,768]{2,1,0:T(8,128)(2,1)}, bf16[192,768]{1,0:T(8,128)(2,1)}) custom-call(s32[768]{0:T(1024)S(1)} %copy-done, bf16[16,12,8,128]{3,2,1,0:T(8,128)(2,1)S(1)} %get-tuple-element.7.from_a, bf16[24,7,8,128]{3,2,1,0:T(8,128)(2,1)S(1)} %get-tuple-element.8.from_b, bf16[192,768]{1,0:T(8,128)(2,1)S(1)} %get-tuple-element.9.solved), custom_call_target="tpu_custom_call" | custom-call | tf_op jit(solution)/shard_map/place/pallas_call | solution.py:452
Async XLA Ops:
  0.6 70.8 %copy-start = (s32[768]{0:T(1024)S(1)}, s32[768]{0:T(1024)}, u32[]{:S(2)}) copy-start(s32[768]{0:T(1024)} %waves.1) | copy-start | bytes 9220
